TPU v7x, 32 devices: a whole 2x2x4 slice. The times are simulated.
32 devices in a mesh: batch: 16 (over z, y, core), rows: 2 (over x).
Axes of the slice: x: 2, y: 2, z: 4, core: 2. Of those that a mesh axis runs over, the one named last changes fastest.
Arguments:
- block_input: bfloat16 [16, 16, 64, 384], P('batch', 'rows'), may hold values from -6 to 6
- output_grad: bfloat16 [16, 16, 64, 768], P('batch', 'rows'), may hold values from -6 to 6
- conv_weight: float32 [384, 1152], P(None, 'batch'), may hold values from -12 to 12
- conv_gain: float32 [384], replicated, may hold values from 0.1 to 1.9
- conv_momentum: float32 [384, 1152], P(None, 'batch'), may hold values from -0.6 to 0.6
- proj_weight: float32 [768, 384], P(None, 'batch'), may hold values from -12 to 12
- proj_gain: float32 [768], replicated, may hold values from 0.1 to 1.9
- proj_momentum: float32 [768, 384], P(None, 'batch'), may hold values from -0.6 to 0.6
Outputs:
- input_grad: bfloat16 [16, 16, 64, 384], P('batch', 'rows')
- new_conv_weight: float32 [384, 1152], P(None, 'batch')
- new_conv_momentum: float32 [384, 1152], P(None, 'batch')
- new_proj_weight: float32 [768, 384], P(None, 'batch')
- new_proj_momentum: float32 [768, 384], P(None, 'batch')
All inputs are finite; a program needn't handle non-finite values.
Results may differ from a plain program's by a relative error of at most 0.0031.
The roundings to bfloat16 on the way count: a program that leaves them out, or rounds other values in their place, can miss the bound.
Values may be sent and summed in bfloat16 or wider, within the bound.
A program may use at most 64 MiB of HBM per device.

v0:
```python
import functools
import math

import jax
import jax.numpy as jnp
from jax import lax
from jax.experimental import pallas as pl
from jax.experimental.pallas import tpu as pltpu
from jax.sharding import PartitionSpec as P

ws_eps = 0.0001
clip_ratio = 0.05
momentum_rate = 0.9
learn_rate = 1.6
norm_eps = 1e-06

F32 = jnp.float32
BF16 = jnp.bfloat16
MESH = pl.DeviceIdType.MESH
TAPS = 3
C0 = math.sqrt(2.0 / math.pi)
C1 = 0.044715


def gelu_parts(x):
    t = jnp.tanh(C0 * (x + C1 * (x * x * x)))
    half = 0.5 * (1.0 + t)
    slope = half + (0.5 * C0) * x * (1.0 - t * t) * (1.0 + (3.0 * C1) * (x * x))
    return x * half, slope


def dot_nn(a, b):
    return jnp.dot(a, b, preferred_element_type=F32)


def dot_nt(a, b):
    return lax.dot_general(a, b, (((1,), (1,)), ((), ())), preferred_element_type=F32)


def dot_tn(a, b):
    return lax.dot_general(a, b, (((0,), (0,)), ((), ())), preferred_element_type=F32)


def bit_of(me, k):
    return (me // 2**k) % 2


def partner_of(me, k):
    return me + (1 - 2 * bit_of(me, k)) * 2**k


def greet_signal(n):
    me = lax.axis_index("batch")
    r = lax.axis_index("rows")
    barrier = pltpu.get_barrier_semaphore()
    for d in range(1, n):
        pl.semaphore_signal(
            barrier, inc=1, device_id={"batch": (me + d) % n}, device_id_type=MESH
        )
    pl.semaphore_signal(barrier, inc=1, device_id={"rows": 1 - r}, device_id_type=MESH)


def greet_wait(n):
    pl.semaphore_wait(pltpu.get_barrier_semaphore(), n)


def push_start(n, me, src, slots, send, recv):
    copies = []
    for d in range(1, n):
        copy = pltpu.make_async_remote_copy(
            src_ref=src,
            dst_ref=slots.at[me],
            send_sem=send.at[d - 1],
            recv_sem=recv.at[d - 1],
            device_id={"batch": (me + d) % n},
            device_id_type=MESH,
        )
        copy.start()
        copies.append(copy)
    for row in range(src.shape[0]):
        slots[me, row] = src[row]
    return copies


def merged(n, slots, at, at_sq, counts, fan):
    total = slots[0, at]
    for i in range(1, n):
        total = total + slots[i, at]
    mean = total / fan
    spread = None
    for i in range(n):
        off = slots[i, at] / counts - mean
        term = slots[i, at_sq] + counts * (off * off)
        spread = term if spread is None else spread + term
    return total, mean, spread


LANE = 128


def kind_slices(ch, out):
    return [(0, 0)] + [(1, b * ch) for b in range(out // ch)]


def gather_kernel(n, nb, pieces, edge_x, edge_u, wc_ref, wp_ref, gc_ref, gp_ref, x_ref, u_ref,
                  full_ref, stat_ref, hx_ref, hu_ref,
                  src, slots, s_send, s_recv, g_send, g_recv, h_send, h_recv):
    me = lax.axis_index("batch")
    r = lax.axis_index("rows")
    greet_signal(n)
    ch = wc_ref.shape[1]
    kinds = kind_slices(ch, wp_ref.shape[1])
    nk = len(kinds)
    w_refs = (wc_ref, wp_ref)
    gain_refs = (gc_ref, gp_ref)
    for b, (which, col) in enumerate(kinds):
        piece = w_refs[which][:, col : col + ch]
        s = jnp.sum(piece, axis=0, keepdims=True)
        cent = piece - s / piece.shape[0]
        src[b] = s
        src[nk + b] = jnp.sum(cent * cent, axis=0, keepdims=True)
    greet_wait(n)
    push = push_start(n, me, src, slots, s_send, s_recv)
    halos = []
    for at, (ref, out, width) in enumerate(((x_ref, hx_ref, edge_x), (u_ref, hu_ref, edge_u))):
        first = (1 - r) * (ref.shape[0] - width)
        copy = pltpu.make_async_remote_copy(
            src_ref=ref.at[pl.ds(first, width)],
            dst_ref=out,
            send_sem=h_send.at[at],
            recv_sem=h_recv.at[at],
            device_id={"rows": 1 - r},
            device_id_type=MESH,
        )
        copy.start()
        halos.append(copy)
    for copy in push:
        copy.wait()
    pos = 0
    for k in range(nb):
        pos = pos + bit_of(me, k) * 2 ** (nb - 1 - k)
    stat_ref[...] = jnp.zeros_like(stat_ref)
    first = 0
    for b, (which, col) in enumerate(kinds):
        count = w_refs[which].shape[0]
        _, mean, spread = merged(n, slots, b, nk + b, count, n * count)
        stat_ref[b : b + 1] = mean
        stat_ref[nk + b : nk + b + 1] = spread
        scale = gain_refs[which][col : col + ch][None] * lax.rsqrt(spread + ws_eps)
        std = (scale * (w_refs[which][:, col : col + ch] - mean)).astype(BF16)
        for p in range(pieces):
            full_ref[p, pos, first : first + count] = std[:, p * LANE : (p + 1) * LANE]
        first += count
    flight = [None] * pieces
    for t in range(nb + pieces):
        for p in range(pieces):
            step = t - p
            if step < 0 or step > nb:
                continue
            if flight[p] is not None:
                flight[p].wait()
            if step == nb:
                continue
            size = 2**step
            base = (pos // size) * size
            flight[p] = pltpu.make_async_remote_copy(
                src_ref=full_ref.at[p, pl.ds(base, size)],
                dst_ref=full_ref.at[p, pl.ds(base, size)],
                send_sem=g_send.at[p, step],
                recv_sem=g_recv.at[p, step],
                device_id={"batch": partner_of(me, nb - 1 - step)},
                device_id_type=MESH,
            )
            flight[p].start()
    for copy in halos:
        copy.wait()


def reduce_kernel(n, nb, pieces, images, part_ref, wc_ref, wp_ref, stat_ref,
                  gc_ref, gp_ref, grad_ref, coef_ref, *scratch):
    recvs = scratch[:nb]
    accs = scratch[nb : 2 * nb]
    recv_x, src, slots, r_send, r_recv, s_send, s_recv, x_send, x_recv = scratch[2 * nb :]
    me = lax.axis_index("batch")
    r = lax.axis_index("rows")
    greet_signal(n)
    greet_wait(n)
    flight = [None] * pieces
    for t in range(nb + 1 + pieces):
        for p in range(pieces):
            k = t - p
            if k < 0 or k > nb + 1:
                continue
            if flight[p] is not None:
                flight[p].wait()
            if 1 <= k <= nb:
                h = n >> k
                cur = part_ref if k == 1 else accs[k - 2]
                acc = accs[k - 1]
                rec = recvs[k - 1]
                lo = bit_of(me, k - 1) * h

                def add(i, carry, cur=cur, acc=acc, rec=rec, lo=lo, p=p):
                    acc[p, i] = (cur[p, lo + i].astype(F32) + rec[p, i].astype(F32)).astype(acc.dtype)
                    return carry

                lax.fori_loop(0, h, add, 0)
            if k < nb:
                h = n >> (k + 1)
                cur = part_ref if k == 0 else accs[k - 1]
                flight[p] = pltpu.make_async_remote_copy(
                    src_ref=cur.at[p, pl.ds((1 - bit_of(me, k)) * h, h)],
                    dst_ref=recvs[k].at[p],
                    send_sem=r_send.at[p, k],
                    recv_sem=r_recv.at[p, k],
                    device_id={"batch": partner_of(me, k)},
                    device_id_type=MESH,
                )
                flight[p].start()
            elif k == nb:
                flight[p] = pltpu.make_async_remote_copy(
                    src_ref=accs[nb - 1].at[p],
                    dst_ref=recv_x.at[p],
                    send_sem=x_send.at[p],
                    recv_sem=x_recv.at[p],
                    device_id={"rows": 1 - r},
                    device_id_type=MESH,
                )
                flight[p].start()
    last = accs[nb - 1]
    grad = jnp.concatenate([last[p, 0] + recv_x[p, 0] for p in range(pieces)], axis=1) / images
    grad_ref[...] = grad
    coef_ref[...] = jnp.zeros_like(coef_ref)
    ch = wc_ref.shape[1]
    kinds = kind_slices(ch, wp_ref.shape[1])
    nk = len(kinds)
    w_refs = (wc_ref, wp_ref)
    gain_refs = (gc_ref, gp_ref)
    first = 0
    for b, (which, col) in enumerate(kinds):
        count = w_refs[which].shape[0]
        piece = grad[first : first + count]
        first += count
        cent = w_refs[which][:, col : col + ch] - stat_ref[b : b + 1]
        s = jnp.sum(piece, axis=0, keepdims=True)
        off = piece - s / count
        src[b] = s
        src[nk + b] = jnp.sum(off * off, axis=0, keepdims=True)
        src[2 * nk + b] = jnp.sum(piece * cent, axis=0, keepdims=True)
    for copy in push_start(n, me, src, slots, s_send, s_recv):
        copy.wait()
    for b, (which, col) in enumerate(kinds):
        count = w_refs[which].shape[0]
        cols = slice(col, col + ch)
        fan = n * count
        _, gmean, gspread = merged(n, slots, b, nk + b, count, fan)
        at = 2 * nk + b
        proj = slots[0, at]
        for i in range(1, n):
            proj = proj + slots[i, at]
        mean = stat_ref[b : b + 1]
        spread = stat_ref[nk + b : nk + b + 1]
        factor = lax.rsqrt(spread + ws_eps)
        f2 = factor * factor
        one = gain_refs[which][cols][None] * factor
        two = one * f2 * proj
        grad_sq = one * one * jnp.maximum(gspread - f2 * proj * proj * (2.0 - f2 * spread), 0.0)
        weight_sq = spread + fan * (mean * mean)
        clip = jnp.minimum(1.0, clip_ratio * jnp.sqrt(weight_sq) * lax.rsqrt(grad_sq + norm_eps))
        coef_ref[b : b + 1] = clip * one
        coef_ref[nk + b : nk + b + 1] = gmean
        coef_ref[2 * nk + b : 2 * nk + b + 1] = clip * two


def update_kernel(grad_ref, coef_ref, stat_ref, wc_ref, wp_ref, mc_ref, mp_ref,
                  nwc_ref, nwp_ref, nmc_ref, nmp_ref):
    ch = wc_ref.shape[1]
    kinds = kind_slices(ch, wp_ref.shape[1])
    nk = len(kinds)
    first = 0
    for b, (which, col) in enumerate(kinds):
        w_ref = (wc_ref, wp_ref)[which]
        count = w_ref.shape[0]
        cols = slice(col, col + ch)
        w = w_ref[:, cols]
        grad = grad_ref[first : first + count]
        first += count
        clipped = coef_ref[b : b + 1] * (grad - coef_ref[nk + b : nk + b + 1]) - coef_ref[
            2 * nk + b : 2 * nk + b + 1
        ] * (w - stat_ref[b : b + 1])
        new_m = momentum_rate * (mc_ref, mp_ref)[which][:, cols] + clipped
        (nmc_ref, nmp_ref)[which][:, cols] = new_m
        (nwc_ref, nwp_ref)[which][:, cols] = w - learn_rate * (clipped + momentum_rate * new_m)


def shifted(vals, step, mc):
    rows = vals.shape[0]
    col = lax.broadcasted_iota(jnp.int32, vals.shape, 0)
    if step > 0:
        return jnp.where(col == mc - 1, 0.0, pltpu.roll(vals, rows - 1, 0))
    return jnp.where(col == 0, 0.0, pltpu.roll(vals, 1, 0))


def compute_kernel(n, order, mr, mc, gw, nc, np_, nblk,
                   x_ref, u_ref, hx_ref, hu_ref, full_ref,
                   ig_ref, part_ref,
                   kt, pt, xs, ys, hid, cg, pg):
    ch = x_ref.shape[1]
    groups = ch // gw
    wide = TAPS * gw
    px = mr * mc
    r = lax.axis_index("rows")
    for d in range(n):
        for p in range(ch // LANE):
            kt[d * nc : (d + 1) * nc, p * LANE : (p + 1) * LANE] = full_ref[p, order[d], :nc]
            for b in range(nblk):
                at = b * ch + p * LANE
                pt[d * np_ : (d + 1) * np_, at : at + LANE] = full_ref[
                    p, order[d], nc + b * np_ : nc + (b + 1) * np_
                ]

    def place(at, vals):
        act = gelu_parts(vals)[0].astype(BF16).astype(F32)
        for j in range(TAPS):
            moved = act if j == 1 else shifted(act, j - 1, mc)
            moved = moved.astype(BF16)
            for g in range(groups):
                xs[pl.ds(at, mc), g * wide + j * gw : g * wide + (j + 1) * gw] = moved[
                    :, g * gw : (g + 1) * gw
                ]

    for e in range(2):
        edge = hx_ref[e * mc : (e + 1) * mc].astype(F32)
        place(e * mc, jnp.where(r == 1, edge, 0.0))
        place((mr + 2 + e) * mc, jnp.where(r == 0, edge, 0.0))

    def body(row, carry):
        at = pl.multiple_of(row * mc, mc)
        place(pl.multiple_of(at + 2 * mc, mc), x_ref[pl.ds(at, mc)].astype(F32))
        return carry

    lax.fori_loop(0, mr, body, 0)

    def forward(e, up):
        hg = dot_nt(up, pt[...])
        for g in range(groups):
            acc = None
            for i in range(TAPS):
                term = dot_nn(
                    xs[pl.ds(pl.multiple_of((e + i) * mc, mc), up.shape[0]), g * wide : (g + 1) * wide],
                    kt[i * wide : (i + 1) * wide, g * gw : (g + 1) * gw],
                )
                acc = term if acc is None else acc + term
            h, slope = gelu_parts(acc)
            hid[pl.ds(pl.multiple_of(e * mc, mc), up.shape[0]), g * gw : (g + 1) * gw] = h.astype(BF16)
            grad = (hg[:, g * gw : (g + 1) * gw] * slope).astype(BF16).astype(F32)
            for q in range(up.shape[0] // mc):
                here = grad[q * mc : (q + 1) * mc]
                for j in range(TAPS):
                    moved = here if j == 1 else shifted(here, 1 - j, mc)
                    ys[pl.ds(pl.multiple_of((e + q) * mc, mc), mc), g * wide + j * gw : g * wide + (j + 1) * gw] = moved.astype(BF16)

    edge = hu_ref[...].astype(F32)
    forward(0, jnp.where(r == 1, edge, 0.0).astype(BF16))
    forward(mr + 1, jnp.where(r == 0, edge, 0.0).astype(BF16))
    many = 2 if mr % 2 == 0 else 1

    def fwd(t, carry):
        up = u_ref[pl.ds(pl.multiple_of(t * many * mc, mc), many * mc)]
        forward(1 + t * many, up)
        return carry

    lax.fori_loop(0, mr // many, fwd, 0)

    pg[...] = dot_tn(hid[mc : mc + px], u_ref[...])
    for g in range(groups):
        own = ys[mc : mc + px, g * wide + gw : g * wide + 2 * gw]
        for i in range(TAPS):
            cg[i * wide : (i + 1) * wide, g * gw : (g + 1) * gw] = dot_tn(
                xs[(1 + i) * mc : (1 + i) * mc + px, g * wide : (g + 1) * wide], own
            )
    for d in range(n):
        for p in range(ch // LANE):
            part_ref[p, order[d], :nc] = cg[
                d * nc : (d + 1) * nc, p * LANE : (p + 1) * LANE
            ].astype(BF16)
            for b in range(nblk):
                at = b * ch + p * LANE
                part_ref[p, order[d], nc + b * np_ : nc + (b + 1) * np_] = pg[
                    d * np_ : (d + 1) * np_, at : at + LANE
                ].astype(BF16)

    def back(t, carry):
        at = pl.multiple_of(t * many * mc, mc)
        for g in range(groups):
            acc = None
            for i in range(TAPS):
                for j in range(TAPS):
                    term = dot_nt(
                        ys[pl.ds(pl.multiple_of(at + (2 - i) * mc, mc), many * mc), g * wide + j * gw : g * wide + (j + 1) * gw],
                        kt[i * wide + j * gw : i * wide + (j + 1) * gw, g * gw : (g + 1) * gw],
                    )
                    acc = term if acc is None else acc + term
            slope = gelu_parts(x_ref[pl.ds(at, many * mc), g * gw : (g + 1) * gw].astype(F32))[1]
            ig_ref[pl.ds(at, many * mc), g * gw : (g + 1) * gw] = (acc * slope).astype(BF16)
        return carry

    lax.fori_loop(0, mr // many, back, 0)


def local(n, nrows, block_input, output_grad, conv_weight, conv_gain, conv_momentum,
          proj_weight, proj_gain, proj_momentum):
    assert nrows == 2
    nb = n.bit_length() - 1
    assert 2**nb == n
    _, mr, mc, ch = block_input.shape
    out = output_grad.shape[3]
    nc = conv_weight.shape[1]
    np_ = proj_weight.shape[1]
    nblk = out // ch
    gw = nc * n // (TAPS * TAPS)
    rows = nc + nblk * np_
    kinds = 1 + nblk
    pieces = ch // LANE
    order = [int(format(d, "0%db" % nb)[::-1], 2) for d in range(n)]
    px = mr * mc

    wc, wp, mc_, mp = conv_weight.T, proj_weight.T, conv_momentum.T, proj_momentum.T
    gc, gp = conv_gain, proj_gain
    x = block_input.reshape(px, ch)
    u = output_grad.reshape(px, out)
    vmem = pl.BlockSpec(memory_space=pltpu.VMEM)
    sdt = jax.ShapeDtypeStruct
    stat_rows = -(-2 * kinds // 8) * 8
    grad_rows = -(-3 * kinds // 8) * 8
    dma = pltpu.SemaphoreType.DMA
    full, stat, hx, hu = pl.pallas_call(
        functools.partial(gather_kernel, n, nb, pieces, 2 * mc, mc),
        out_shape=(
            sdt((pieces, n, rows, LANE), BF16),
            sdt((stat_rows, ch), F32),
            sdt((2 * mc, ch), BF16),
            sdt((mc, out), BF16),
        ),
        in_specs=[vmem] * 6,
        out_specs=(vmem,) * 4,
        scratch_shapes=[
            pltpu.VMEM((2 * kinds, 1, ch), F32),
            pltpu.VMEM((n, 2 * kinds, 1, ch), F32),
            dma((n - 1,)), dma((n - 1,)),
            dma((pieces, nb)), dma((pieces, nb)),
            dma((2,)), dma((2,)),
        ],
        compiler_params=pltpu.CompilerParams(collective_id=0, has_side_effects=True),
        name="gather",
    )(wc, wp, gc, gp, x, u)
    ig, part = pl.pallas_call(
        functools.partial(compute_kernel, n, order, mr, mc, gw, nc, np_, nblk),
        out_shape=(sdt((px, ch), BF16), sdt((pieces, n, rows, LANE), BF16)),
        in_specs=[vmem] * 5,
        out_specs=(vmem,) * 2,
        scratch_shapes=[
            pltpu.VMEM((n * nc, ch), BF16),
            pltpu.VMEM((n * np_, out), BF16),
            pltpu.VMEM(((mr + 4) * mc, TAPS * ch), BF16),
            pltpu.VMEM(((mr + 2) * mc, TAPS * ch), BF16),
            pltpu.VMEM(((mr + 2) * mc, ch), BF16),
            pltpu.VMEM((n * nc, ch), F32),
            pltpu.VMEM((n * np_, out), F32),
        ],
        name="compute",
    )(x, u, hx, hu, full)
    halves = [n >> (k + 1) for k in range(nb)]
    grad, coef = pl.pallas_call(
        functools.partial(reduce_kernel, n, nb, pieces, n),
        out_shape=(sdt((rows, ch), F32), sdt((grad_rows, ch), F32)),
        in_specs=[vmem] * 6,
        out_specs=(vmem,) * 2,
        scratch_shapes=[pltpu.VMEM((pieces, h, rows, LANE), BF16) for h in halves]
        + [pltpu.VMEM((pieces, h, rows, LANE), BF16 if h > 1 else F32) for h in halves]
        + [
            pltpu.VMEM((pieces, 1, rows, LANE), F32),
            pltpu.VMEM((3 * kinds, 1, ch), F32),
            pltpu.VMEM((n, 3 * kinds, 1, ch), F32),
            dma((pieces, nb)), dma((pieces, nb)),
            dma((n - 1,)), dma((n - 1,)),
            dma((pieces,)), dma((pieces,)),
        ],
        compiler_params=pltpu.CompilerParams(collective_id=1, has_side_effects=True),
        name="reduce",
    )(part, wc, wp, stat, gc, gp)
    nwc, nwp, nmc, nmp = pl.pallas_call(
        update_kernel,
        out_shape=(sdt((nc, ch), F32), sdt((np_, out), F32)) * 2,
        in_specs=[vmem] * 7,
        out_specs=(vmem,) * 4,
        name="update",
    )(grad, coef, stat, wc, wp, mc_, mp)
    return (ig.reshape(block_input.shape), nwc.T, nmc.T, nwp.T, nmp.T)


def solution(mesh):
    in_specs = (
        P("batch", "rows", None, None),
        P("batch", "rows", None, None),
        P(None, "batch"),
        P(),
        P(None, "batch"),
        P(None, "batch"),
        P(),
        P(None, "batch"),
    )
    out_specs = (
        P("batch", "rows", None, None),
        P(None, "batch"),
        P(None, "batch"),
        P(None, "batch"),
        P(None, "batch"),
    )
    body = functools.partial(local, mesh.shape["batch"], mesh.shape["rows"])
    return jax.shard_map(body, mesh=mesh, in_specs=in_specs, out_specs=out_specs, check_vma=False)
```

profile of v0, /device:TPU:0, one launch (start us, length us, event | category | flops | bytes accessed | tf_op | source)
XLA Modules:
  0.0 83.4 jit_solution(17638194929125096658)
XLA Ops:
  0.6 35.0 %gather.1 = (bf16[3,16,120,128]{3,2,1,0:T(8,128)(2,1)}, f32[8,384]{1,0:T(8,128)}, bf16[128,384]{1,0:T(8,128)(2,1)}, bf16[64,768]{1,0:T(8,128)(2,1)}) custom-call(f32[72,384]{1,0:T(8,128)} %bitcast.15, f32[24,768]{1,0:T(8,128)} %bitcast.18, f32[384]{0:T(512)} %gc_ref.3, f32[768]{0:T(1024)} %gp_ref.3, bf16[512,384]{1,0:T(8,128)(2,1)} %bitcast.13, ...), custom_call_target="tpu_custom_call" | custom-call | tf_op jit(solution)/shard_map/gather/pallas_call | solution.py:437
  35.7 11.1 %compute.1 = (bf16[512,384]{1,0:T(8,128)(2,1)}, bf16[3,16,120,128]{3,2,1,0:T(8,128)(2,1)}) custom-call(bf16[512,384]{1,0:T(8,128)(2,1)} %bitcast.14, bf16[512,768]{1,0:T(8,128)(2,1)} %bitcast.12, bf16[128,384]{1,0:T(8,128)(2,1)} %get-tuple-element.17.hx_ref, bf16[64,768]{1,0:T(8,128)(2,1)} %get-tuple-element.18.hu_ref, ...), custom_call_target="tpu_custom_call" | custom-call | tf_op jit(solution)/shard_map/compute/pallas_call | solution.py:457
  46.8 34.7 %reduce.1 = (f32[120,384]{1,0:T(8,128)}, f32[16,384]{1,0:T(8,128)}) custom-call(bf16[3,16,120,128]{3,2,1,0:T(8,128)(2,1)} %get-tuple-element.21.part_ref, f32[72,384]{1,0:T(8,128)} %bitcast.16, f32[24,768]{1,0:T(8,128)} %bitcast.19, f32[8,384]{1,0:T(8,128)} %get-tuple-element.22.stat_ref, f32[384]{0:T(512)} %gc_ref.3, f32[768]{0:T(1024)} %gp_ref.3), custom_call_target="tpu_custom_call" | custom-call | tf_op jit(solution)/shard_map/reduce/pallas_call | solution.py:474
  81.5 1.9 %update.1 = (f32[72,384]{1,0:T(8,128)}, f32[24,768]{1,0:T(8,128)}, f32[72,384]{1,0:T(8,128)}, f32[24,768]{1,0:T(8,128)}) custom-call(f32[120,384]{1,0:T(8,128)} %get-tuple-element.23.grad_ref, f32[16,384]{1,0:T(8,128)} %get-tuple-element.24.coef_ref, f32[8,384]{1,0:T(8,128)} %get-tuple-element.22.stat_ref, f32[72,384]{1,0:T(8,128)} %bitcast.17, ...), custom_call_target="tpu_custom_call" | custom-call | tf_op jit(solution)/shard_map/update/pallas_call | solution.py:492
where the time goes:
time: 83.7 us; the launch traced here: 83.4 us
  Pallas kernels  82.8 us (99%)
    pallas_call x1, Pallas kernels, local(): pl.pallas_call(functools.partial(gather_kernel, n, nb, pieces, 2 * mc, mc...  35 us
    pallas_call x1, Pallas kernels, local(): pl.pallas_call(functools.partial(reduce_kernel, n, nb, pieces, n), out_sh...  34.7 us
    pallas_call x1, Pallas kernels, local(): pl.pallas_call(functools.partial(compute_kernel, n, order, mr, mc, gw, nc...  11.1 us
    pallas_call x1, Pallas kernels, local(): pl.pallas_call(update_kernel, out_shape=(sdt((nc, ch), F32), sdt((np_, ou...  1.92 us

commit v1 on v0

v1 whole, which is shorter than its diff:
```python
import functools
import math

import jax
import jax.numpy as jnp
from jax import lax
from jax.experimental import pallas as pl
from jax.experimental.pallas import tpu as pltpu
from jax.sharding import PartitionSpec as P

ws_eps = 0.0001
clip_ratio = 0.05
momentum_rate = 0.9
learn_rate = 1.6
norm_eps = 1e-06

F32 = jnp.float32
BF16 = jnp.bfloat16
MESH = pl.DeviceIdType.MESH
TAPS = 3
C0 = math.sqrt(2.0 / math.pi)
C1 = 0.044715


def gelu_parts(x):
    t = jnp.tanh(C0 * (x + C1 * (x * x * x)))
    half = 0.5 * (1.0 + t)
    slope = half + (0.5 * C0) * x * (1.0 - t * t) * (1.0 + (3.0 * C1) * (x * x))
    return x * half, slope


def dot_nn(a, b):
    return jnp.dot(a, b, preferred_element_type=F32)


def dot_nt(a, b):
    return lax.dot_general(a, b, (((1,), (1,)), ((), ())), preferred_element_type=F32)


def dot_tn(a, b):
    return lax.dot_general(a, b, (((0,), (0,)), ((), ())), preferred_element_type=F32)


LANE = 128


class Plan:
    def __init__(self, n, ch, out, nc, np_):
        nb = n.bit_length() - 1
        assert 2**nb == n and nb >= 1
        self.n, self.nc, self.np_ = n, nc, np_
        self.nz = 2 ** (nb // 2)
        self.nm = n // 2 // self.nz
        self.half = n // 2
        self.ch, self.out = ch, out
        self.nblk = out // ch
        self.pieces = ch // LANE
        cut = self.pieces // 2
        rest = self.pieces - cut
        self.sets = (
            [("q", k) for k in range(cut)] + [("c", k) for k in range(rest)],
            [("q", k) for k in range(cut, self.pieces)] + [("c", k) for k in range(rest, self.pieces)],
        )
        self.tiles = tuple([t for chunk in one for t in self.tiles_of(chunk)] for one in self.sets)
        self.wide = max(len(t) for t in self.tiles)
        assert self.wide <= 5
        self.proj_tiles = tuple(sum(which for which, _ in one) for one in self.tiles)

    def tiles_of(self, chunk):
        kind, k = chunk
        if kind == "c":
            return [(0, k * LANE)]
        return [(1, b * self.ch + k * LANE) for b in range(self.nblk)]

    def count_of(self, which):
        return self.np_ if which else self.nc

    def chunk_rows(self, kind):
        return self.nc if kind == "c" else self.nblk * self.np_

    def slot(self, d):
        return (d % 2 * self.nm + d // 2 % self.nm) * self.nz + d // 2 // self.nm

    def place(self, me):
        return me % 2, me // 2 % self.nm, me // 2 // self.nm

    def batch(self, c, m, z):
        return (z * self.nm + m) * 2 + c


def send(src, dst, sems, at, where):
    return pltpu.make_async_remote_copy(
        src_ref=src, dst_ref=dst, send_sem=sems[0].at[at], recv_sem=sems[1].at[at],
        device_id=where, device_id_type=MESH,
    )


def greet(plan):
    me = lax.axis_index("batch")
    r = lax.axis_index("rows")
    c, m, z = plan.place(me)
    n = plan.n
    barrier = pltpu.get_barrier_semaphore()
    for d in range(1, n):
        pl.semaphore_signal(barrier, inc=1, device_id={"batch": (me + d) % n}, device_id_type=MESH)
    for j in range(plan.nm):
        to = plan.batch(c, (m + j) % plan.nm, z)
        pl.semaphore_signal(barrier, inc=1, device_id={"batch": to, "rows": 1 - r}, device_id_type=MESH)


def greet_wait(plan):
    pl.semaphore_wait(pltpu.get_barrier_semaphore(), plan.n - 1 + plan.nm)


def push_all(plan, me, src, slots, sems):
    n = plan.n
    copies = []
    for d in range(1, n):
        copy = send(src, slots.at[me], sems, d - 1, {"batch": (me + d) % n})
        copy.start()
        copies.append(copy)
    slots[me] = src[...]
    return copies


def counts_of(plan, r):
    row = lax.broadcasted_iota(jnp.int32, (8, LANE), 0)
    first = jnp.where(r == 0, plan.proj_tiles[0], plan.proj_tiles[1])
    return jnp.where(row < first, float(plan.np_), float(plan.nc))


def merged(plan, slots, cnt):
    w = plan.wide
    total = slots[0]
    for i in range(1, plan.n):
        total = total + slots[i]
    mean = total[0:8] / (plan.n * cnt)
    between = None
    for i in range(plan.n):
        off = slots[i, 0:8] / cnt - mean
        term = cnt * (off * off)
        between = term if between is None else between + term
    return total, mean[0:w], total[w : 2 * w] + between[0:w]


def by_half(r, fn):
    for rr in range(2):
        @pl.when(r == rr)
        def _(rr=rr):
            fn(rr)


def gather_kernel(plan, edge_x, edge_u, wc_ref, wp_ref, gc_ref, gp_ref, x_ref, u_ref,
                  fc_ref, fq_ref, stat_ref, hx_ref, hu_ref,
                  src, slots, s_send, s_recv, z_send, z_recv, m_send, m_recv,
                  d_send, d_recv, h_send, h_recv):
    me = lax.axis_index("batch")
    r = lax.axis_index("rows")
    c, m, z = plan.place(me)
    nz, nm, w = plan.nz, plan.nm, plan.wide
    greet(plan)
    w_refs = (wc_ref, wp_ref)
    gain_refs = (gc_ref, gp_ref)
    full = {"c": fc_ref, "q": fq_ref}
    src[...] = jnp.zeros_like(src)

    def local_stats(rr):
        for i, (which, col) in enumerate(plan.tiles[rr]):
            piece = w_refs[which][:, col : col + LANE]
            s = jnp.sum(piece, axis=0, keepdims=True)
            cent = piece - s / piece.shape[0]
            src[i : i + 1] = s
            src[w + i : w + i + 1] = jnp.sum(cent * cent, axis=0, keepdims=True)

    by_half(r, local_stats)
    greet_wait(plan)
    push = push_all(plan, me, src, slots, (s_send, s_recv))
    halos = []
    for at, (ref, out, width) in enumerate(((x_ref, hx_ref, edge_x), (u_ref, hu_ref, edge_u))):
        first = (1 - r) * (ref.shape[0] - width)
        copy = send(ref.at[pl.ds(first, width)], out, (h_send, h_recv), at, {"rows": 1 - r})
        copy.start()
        halos.append(copy)
    for copy in push:
        copy.wait()
    cnt = counts_of(plan, r)
    _, mean, spread = merged(plan, slots, cnt)
    stat_ref[r] = jnp.zeros_like(stat_ref[0])
    stat_ref[r, 0:w] = mean
    stat_ref[r, 8 : 8 + w] = spread
    copy = send(stat_ref.at[r], stat_ref.at[r], (h_send, h_recv), 2, {"rows": 1 - r})
    copy.start()
    halos.append(copy)
    factor = lax.rsqrt(spread + ws_eps)
    slot = (c * nm + m) * nz + z

    def z_copy(k, j, chunk):
        kind, g = chunk
        at = full[kind].at[g, slot]
        return send(at, at, (z_send, z_recv), (k, j - 1), {"batch": plan.batch(c, m, (z + j) % nz)})

    def start_z(rr):
        i = 0
        for k, chunk in enumerate(plan.sets[rr]):
            kind, g = chunk
            for b, (which, col) in enumerate(plan.tiles_of(chunk)):
                count = plan.count_of(which)
                scale = gain_refs[which][col : col + LANE][None] * factor[i : i + 1]
                std = (scale * (w_refs[which][:, col : col + LANE] - mean[i : i + 1])).astype(BF16)
                full[kind][g, slot, b * count : (b + 1) * count] = std
                i += 1
            for j in range(1, nz):
                z_copy(k, j, chunk).start()

    by_half(r, start_z)
    base = (c * nm + m) * nz

    def m_copy(k, j, jx, chunk, rows):
        kind, g = chunk
        at = full[kind].at[g, pl.ds(base, nz)]
        where = {"batch": plan.batch(c, (m + j) % nm, z), "rows": (r + jx) % 2}
        return send(at, at, (m_send, m_recv), (k, jx * nm + j - 1), where)

    peers = [(j, jx) for jx in range(2) for j in range(nm) if (j, jx) != (0, 0)]

    def spread_m(k):
        def fn(rr):
            chunk = plan.sets[rr][k]
            for j in range(1, nz):
                z_copy(k, j, chunk).wait()
            for j, jx in peers:
                m_copy(k, j, jx, chunk, None).start()
        by_half(r, fn)

    def finish_m(k):
        def fn(rr):
            for j, jx in peers:
                m_copy(k, j, jx, plan.sets[rr][k], None).wait_send()
                m_copy(k, j, jx, plan.sets[(rr + jx) % 2][k], None).wait_recv()
        by_half(r, fn)

    def d_copy(k, side):
        kind, g = plan.sets[side][k]
        at = full[kind].at[g, pl.ds(c * plan.half, plan.half)]
        return send(at, at, (d_send, d_recv), (k, side), {"batch": plan.batch(1 - c, m, z)})

    for k in range(plan.pieces):
        spread_m(k)
    for k in range(plan.pieces):
        finish_m(k)
        for side in range(2):
            d_copy(k, side).start()
    for k in range(plan.pieces):
        for side in range(2):
            d_copy(k, side).wait()
    for copy in halos:
        copy.wait()


def reduce_kernel(plan, images, pc_ref, pq_ref, wc_ref, wp_ref, stat_ref, gc_ref, gp_ref,
                  gradc_ref, gradq_ref, coef_ref,
                  dc, dq, ac, aq, mc_, mq, zc, zq, bc, bq, src, slots, gain_s,
                  s_send, s_recv, z_send, z_recv, m_send, m_recv, d_send, d_recv, x_send, x_recv):
    me = lax.axis_index("batch")
    r = lax.axis_index("rows")
    c, m, z = plan.place(me)
    nz, nm, w = plan.nz, plan.nm, plan.wide
    part = {"c": pc_ref, "q": pq_ref}
    got_d = {"c": dc, "q": dq}
    two = {"c": ac, "q": aq}
    got_m = {"c": mc_, "q": mq}
    eight = {"c": bc, "q": bq}
    got_z = {"c": zc, "q": zq}
    grads = {"c": gradc_ref, "q": gradq_ref}
    greet(plan)
    greet_wait(plan)
    order = list(reversed(range(plan.pieces)))

    def d_copy(k, side):
        kind, g = plan.sets[side][k]
        return send(
            part[kind].at[g, pl.ds((1 - c) * plan.half, plan.half)], got_d[kind].at[g],
            (d_send, d_recv), (k, side), {"batch": plan.batch(1 - c, m, z)},
        )

    for k in order:
        for side in range(2):
            d_copy(k, side).start()

    def m_copy(k, j, jx, chunk):
        kind, g = chunk
        to = (m + j) % nm
        return send(
            two[kind].at[g, pl.ds(to * nz, nz)], got_m[kind].at[g, jx * nm + j - 1],
            (m_send, m_recv), (k, jx * nm + j - 1),
            {"batch": plan.batch(c, to, z), "rows": (r + jx) % 2},
        )

    peers = [(j, jx) for jx in (1, 0) for j in reversed(range(nm)) if (j, jx) != (0, 0)]

    def step_m(k):
        for side in range(2):
            d_copy(k, side).wait()

        def fn(rr):
            for j, jx in peers:
                kind, g = plan.sets[(rr + jx) % 2][k]
                first = (m + j) % nm * nz

                def add(i, carry, kind=kind, g=g, first=first):
                    total = part[kind][g, c * plan.half + first + i].astype(F32) + got_d[kind][g, first + i].astype(F32)
                    two[kind][g, first + i] = total.astype(BF16)
                    return carry

                lax.fori_loop(0, nz, add, 0)
                m_copy(k, j, jx, (kind, g)).start()
        by_half(r, fn)

    def z_copy(k, j, chunk):
        kind, g = chunk
        to = (z + j) % nz
        return send(
            eight[kind].at[g, to], got_z[kind].at[g, j - 1],
            (z_send, z_recv), (k, j - 1), {"batch": plan.batch(c, m, to)},
        )

    def sum_m(kind, g, at):
        first = m * nz + at
        total = part[kind][g, c * plan.half + first].astype(F32) + got_d[kind][g, first].astype(F32)
        for i in range(2 * nm - 1):
            total = total + got_m[kind][g, i, at].astype(F32)
        return total

    def step_z(k):
        def fn(rr):
            for j, jx in peers:
                m_copy(k, j, jx, plan.sets[(rr + jx) % 2][k]).wait_send()
                m_copy(k, j, jx, plan.sets[rr][k]).wait_recv()
            kind, g = plan.sets[rr][k]
            for j in range(1, nz):
                to = (z + j) % nz
                eight[kind][g, to] = sum_m(kind, g, to).astype(BF16)
                z_copy(k, j, (kind, g)).start()
            grads[kind][g] = sum_m(kind, g, z)
        by_half(r, fn)

    def x_copy(k, chunk):
        kind, g = chunk
        return send(grads[kind].at[g], grads[kind].at[g], (x_send, x_recv), k, {"rows": 1 - r})

    def finish(k):
        def fn(rr):
            kind, g = plan.sets[rr][k]
            total = grads[kind][g]
            for j in range(1, nz):
                z_copy(k, j, (kind, g)).wait()
                total = total + got_z[kind][g, j - 1].astype(F32)
            grads[kind][g] = total / images
            x_copy(k, (kind, g)).start()
        by_half(r, fn)

    for k in order:
        step_m(k)
    for k in order:
        step_z(k)
    for k in order:
        finish(k)
    w_refs = (wc_ref, wp_ref)
    gain_refs = (gc_ref, gp_ref)
    src[...] = jnp.zeros_like(src)
    gain_s[...] = jnp.zeros_like(gain_s)

    def local_stats(rr):
        i = 0
        for chunk in plan.sets[rr]:
            kind, g = chunk
            for b, (which, col) in enumerate(plan.tiles_of(chunk)):
                count = plan.count_of(which)
                piece = grads[kind][g, b * count : (b + 1) * count]
                cent = w_refs[which][:, col : col + LANE] - stat_ref[rr, i : i + 1]
                s = jnp.sum(piece, axis=0, keepdims=True)
                off = piece - s / count
                src[i : i + 1] = s
                src[w + i : w + i + 1] = jnp.sum(off * off, axis=0, keepdims=True)
                src[2 * w + i : 2 * w + i + 1] = jnp.sum(piece * cent, axis=0, keepdims=True)
                gain_s[i : i + 1] = gain_refs[which][col : col + LANE][None]
                i += 1

    by_half(r, local_stats)
    for copy in push_all(plan, me, src, slots, (s_send, s_recv)):
        copy.wait()
    cnt = counts_of(plan, r)
    total, gmean, gspread = merged(plan, slots, cnt)
    proj = total[2 * w : 3 * w]
    fan = plan.n * cnt[0:w]
    mean = stat_ref[r, 0:w]
    spread = stat_ref[r, 8 : 8 + w]
    factor = lax.rsqrt(spread + ws_eps)
    f2 = factor * factor
    one = gain_s[0:w] * factor
    coef_two = one * f2 * proj
    grad_sq = one * one * jnp.maximum(gspread - f2 * proj * proj * (2.0 - f2 * spread), 0.0)
    weight_sq = spread + fan * (mean * mean)
    clip = jnp.minimum(1.0, clip_ratio * jnp.sqrt(weight_sq) * lax.rsqrt(grad_sq + norm_eps))
    coef_ref[r] = jnp.zeros_like(coef_ref[0])
    coef_ref[r, 0:w] = clip * one
    coef_ref[r, 8 : 8 + w] = gmean
    coef_ref[r, 16 : 16 + w] = clip * coef_two
    last = send(coef_ref.at[r], coef_ref.at[r], (x_send, x_recv), plan.pieces, {"rows": 1 - r})
    last.start()

    def end(rr):
        for k in range(plan.pieces):
            x_copy(k, plan.sets[rr][k]).wait_send()
            x_copy(k, plan.sets[1 - rr][k]).wait_recv()

    by_half(r, end)
    last.wait()


def update_kernel(plan, gradc_ref, gradq_ref, coef_ref, stat_ref, wc_ref, wp_ref, mc_ref, mp_ref,
                  nwc_ref, nwp_ref, nmc_ref, nmp_ref):
    grads = {"c": gradc_ref, "q": gradq_ref}
    for rr in range(2):
        i = 0
        for chunk in plan.sets[rr]:
            kind, g = chunk
            for b, (which, col) in enumerate(plan.tiles_of(chunk)):
                count = plan.count_of(which)
                cols = slice(col, col + LANE)
                w = (wc_ref, wp_ref)[which][:, cols]
                grad = grads[kind][g, b * count : (b + 1) * count]
                clipped = coef_ref[rr, i : i + 1] * (grad - coef_ref[rr, 8 + i : 9 + i]) - coef_ref[
                    rr, 16 + i : 17 + i
                ] * (w - stat_ref[rr, i : i + 1])
                new_m = momentum_rate * (mc_ref, mp_ref)[which][:, cols] + clipped
                (nmc_ref, nmp_ref)[which][:, cols] = new_m
                (nwc_ref, nwp_ref)[which][:, cols] = w - learn_rate * (clipped + momentum_rate * new_m)
                i += 1


def shifted(vals, step, mc):
    rows = vals.shape[0]
    col = lax.broadcasted_iota(jnp.int32, vals.shape, 0)
    if step > 0:
        return jnp.where(col == mc - 1, 0.0, pltpu.roll(vals, rows - 1, 0))
    return jnp.where(col == 0, 0.0, pltpu.roll(vals, 1, 0))


def compute_kernel(plan, mr, mc, gw,
                   x_ref, u_ref, hx_ref, hu_ref, fc_ref, fq_ref,
                   ig_ref, pc_ref, pq_ref,
                   kt, pt, xs, ys, hid, cg, pg):
    n, nc, np_, nblk = plan.n, plan.nc, plan.np_, plan.nblk
    order = [plan.slot(d) for d in range(n)]
    ch = x_ref.shape[1]
    groups = ch // gw
    wide = TAPS * gw
    px = mr * mc
    r = lax.axis_index("rows")
    for d in range(n):
        for p in range(ch // LANE):
            kt[d * nc : (d + 1) * nc, p * LANE : (p + 1) * LANE] = fc_ref[p, order[d]]
            for b in range(nblk):
                at = b * ch + p * LANE
                pt[d * np_ : (d + 1) * np_, at : at + LANE] = fq_ref[
                    p, order[d], b * np_ : (b + 1) * np_
                ]

    def place(at, vals):
        act = gelu_parts(vals)[0].astype(BF16).astype(F32)
        for j in range(TAPS):
            moved = act if j == 1 else shifted(act, j - 1, mc)
            moved = moved.astype(BF16)
            for g in range(groups):
                xs[pl.ds(at, mc), g * wide + j * gw : g * wide + (j + 1) * gw] = moved[
                    :, g * gw : (g + 1) * gw
                ]

    for e in range(2):
        edge = hx_ref[e * mc : (e + 1) * mc].astype(F32)
        place(e * mc, jnp.where(r == 1, edge, 0.0))
        place((mr + 2 + e) * mc, jnp.where(r == 0, edge, 0.0))

    def body(row, carry):
        at = pl.multiple_of(row * mc, mc)
        place(pl.multiple_of(at + 2 * mc, mc), x_ref[pl.ds(at, mc)].astype(F32))
        return carry

    lax.fori_loop(0, mr, body, 0)

    def forward(e, up):
        hg = dot_nt(up, pt[...])
        for g in range(groups):
            acc = None
            for i in range(TAPS):
                term = dot_nn(
                    xs[pl.ds(pl.multiple_of((e + i) * mc, mc), up.shape[0]), g * wide : (g + 1) * wide],
                    kt[i * wide : (i + 1) * wide, g * gw : (g + 1) * gw],
                )
                acc = term if acc is None else acc + term
            h, slope = gelu_parts(acc)
            hid[pl.ds(pl.multiple_of(e * mc, mc), up.shape[0]), g * gw : (g + 1) * gw] = h.astype(BF16)
            grad = (hg[:, g * gw : (g + 1) * gw] * slope).astype(BF16).astype(F32)
            for q in range(up.shape[0] // mc):
                here = grad[q * mc : (q + 1) * mc]
                for j in range(TAPS):
                    moved = here if j == 1 else shifted(here, 1 - j, mc)
                    ys[pl.ds(pl.multiple_of((e + q) * mc, mc), mc), g * wide + j * gw : g * wide + (j + 1) * gw] = moved.astype(BF16)

    edge = hu_ref[...].astype(F32)
    forward(0, jnp.where(r == 1, edge, 0.0).astype(BF16))
    forward(mr + 1, jnp.where(r == 0, edge, 0.0).astype(BF16))
    many = 2 if mr % 2 == 0 else 1

    def fwd(t, carry):
        up = u_ref[pl.ds(pl.multiple_of(t * many * mc, mc), many * mc)]
        forward(1 + t * many, up)
        return carry

    lax.fori_loop(0, mr // many, fwd, 0)

    pg[...] = dot_tn(hid[mc : mc + px], u_ref[...])
    for g in range(groups):
        own = ys[mc : mc + px, g * wide + gw : g * wide + 2 * gw]
        for i in range(TAPS):
            cg[i * wide : (i + 1) * wide, g * gw : (g + 1) * gw] = dot_tn(
                xs[(1 + i) * mc : (1 + i) * mc + px, g * wide : (g + 1) * wide], own
            )
    for d in range(n):
        for p in range(ch // LANE):
            pc_ref[p, order[d]] = cg[
                d * nc : (d + 1) * nc, p * LANE : (p + 1) * LANE
            ].astype(BF16)
            for b in range(nblk):
                at = b * ch + p * LANE
                pq_ref[p, order[d], b * np_ : (b + 1) * np_] = pg[
                    d * np_ : (d + 1) * np_, at : at + LANE
                ].astype(BF16)

    def back(t, carry):
        at = pl.multiple_of(t * many * mc, mc)
        for g in range(groups):
            acc = None
            for i in range(TAPS):
                for j in range(TAPS):
                    term = dot_nt(
                        ys[pl.ds(pl.multiple_of(at + (2 - i) * mc, mc), many * mc), g * wide + j * gw : g * wide + (j + 1) * gw],
                        kt[i * wide + j * gw : i * wide + (j + 1) * gw, g * gw : (g + 1) * gw],
                    )
                    acc = term if acc is None else acc + term
            slope = gelu_parts(x_ref[pl.ds(at, many * mc), g * gw : (g + 1) * gw].astype(F32))[1]
            ig_ref[pl.ds(at, many * mc), g * gw : (g + 1) * gw] = (acc * slope).astype(BF16)
        return carry

    lax.fori_loop(0, mr // many, back, 0)


def local(n, nrows, block_input, output_grad, conv_weight, conv_gain, conv_momentum,
          proj_weight, proj_gain, proj_momentum):
    assert nrows == 2
    _, mr, mc, ch = block_input.shape
    out = output_grad.shape[3]
    nc = conv_weight.shape[1]
    np_ = proj_weight.shape[1]
    gw = nc * n // (TAPS * TAPS)
    plan = Plan(n, ch, out, nc, np_)
    nz, nm, half, pieces = plan.nz, plan.nm, plan.half, plan.pieces
    px = mr * mc
    rq = plan.chunk_rows("q")

    wc, wp, mc_, mp = conv_weight.T, proj_weight.T, conv_momentum.T, proj_momentum.T
    gc, gp = conv_gain, proj_gain
    x = block_input.reshape(px, ch)
    u = output_grad.reshape(px, out)
    vmem = pl.BlockSpec(memory_space=pltpu.VMEM)
    sdt = jax.ShapeDtypeStruct
    dma = pltpu.SemaphoreType.DMA

    def pair(shape):
        return [dma(shape), dma(shape)]

    def both(*lead, dtype=BF16):
        return [pltpu.VMEM((pieces, *lead, nc, LANE), dtype), pltpu.VMEM((pieces, *lead, rq, LANE), dtype)]

    whole = (sdt((pieces, n, nc, LANE), BF16), sdt((pieces, n, rq, LANE), BF16))
    fc, fq, stat, hx, hu = pl.pallas_call(
        functools.partial(gather_kernel, plan, 2 * mc, mc),
        out_shape=whole + (
            sdt((2, 16, LANE), F32),
            sdt((2 * mc, ch), BF16),
            sdt((mc, out), BF16),
        ),
        in_specs=[vmem] * 6,
        out_specs=(vmem,) * 5,
        scratch_shapes=[pltpu.VMEM((16, LANE), F32), pltpu.VMEM((n, 16, LANE), F32)]
        + pair((n - 1,)) + pair((pieces, max(nz - 1, 1))) + pair((pieces, 2 * nm - 1))
        + pair((pieces, 2)) + pair((3,)),
        compiler_params=pltpu.CompilerParams(collective_id=0, has_side_effects=True),
        name="gather",
    )(wc, wp, gc, gp, x, u)
    ig, pc, pq = pl.pallas_call(
        functools.partial(compute_kernel, plan, mr, mc, gw),
        out_shape=(sdt((px, ch), BF16),) + whole,
        in_specs=[vmem] * 6,
        out_specs=(vmem,) * 3,
        scratch_shapes=[
            pltpu.VMEM((n * nc, ch), BF16),
            pltpu.VMEM((n * np_, out), BF16),
            pltpu.VMEM(((mr + 4) * mc, TAPS * ch), BF16),
            pltpu.VMEM(((mr + 2) * mc, TAPS * ch), BF16),
            pltpu.VMEM(((mr + 2) * mc, ch), BF16),
            pltpu.VMEM((n * nc, ch), F32),
            pltpu.VMEM((n * np_, out), F32),
        ],
        name="compute",
    )(x, u, hx, hu, fc, fq)
    gradc, gradq, coef = pl.pallas_call(
        functools.partial(reduce_kernel, plan, n),
        out_shape=(sdt((pieces, nc, LANE), F32), sdt((pieces, rq, LANE), F32), sdt((2, 24, LANE), F32)),
        in_specs=[vmem] * 7,
        out_specs=(vmem,) * 3,
        scratch_shapes=both(half) + both(half) + both(2 * nm - 1, nz) + both(max(nz - 1, 1)) + both(nz)
        + [pltpu.VMEM((16, LANE), F32), pltpu.VMEM((n, 16, LANE), F32), pltpu.VMEM((8, LANE), F32)]
        + pair((n - 1,)) + pair((pieces, max(nz - 1, 1))) + pair((pieces, 2 * nm - 1))
        + pair((pieces, 2)) + pair((pieces + 1,)),
        compiler_params=pltpu.CompilerParams(collective_id=1, has_side_effects=True),
        name="reduce",
    )(pc, pq, wc, wp, stat, gc, gp)
    nwc, nwp, nmc, nmp = pl.pallas_call(
        functools.partial(update_kernel, plan),
        out_shape=(sdt((nc, ch), F32), sdt((np_, out), F32)) * 2,
        in_specs=[vmem] * 8,
        out_specs=(vmem,) * 4,
        name="update",
    )(gradc, gradq, coef, stat, wc, wp, mc_, mp)
    return (ig.reshape(block_input.shape), nwc.T, nmc.T, nwp.T, nmp.T)


def solution(mesh):
    in_specs = (
        P("batch", "rows", None, None),
        P("batch", "rows", None, None),
        P(None, "batch"),
        P(),
        P(None, "batch"),
        P(None, "batch"),
        P(),
        P(None, "batch"),
    )
    out_specs = (
        P("batch", "rows", None, None),
        P(None, "batch"),
        P(None, "batch"),
        P(None, "batch"),
        P(None, "batch"),
    )
    body = functools.partial(local, mesh.shape["batch"], mesh.shape["rows"])
    return jax.shard_map(body, mesh=mesh, in_specs=in_specs, out_specs=out_specs, check_vma=False)
```

time: 83.7 us -> 69.7 us (0.83)
  Pallas kernels: 82.8 us -> 68.8 us
    pallas_call x4, Pallas kernels: 82.8 us -> 68.8 us  [the longest x1 29.2 us: local(): pl.pallas_call(functools.partial(gather_kernel, plan, 2 * mc, mc), out_sh...]
where the time goes in v1:
time: 69.7 us; the launch traced here: 69.4 us
  Pallas kernels  68.8 us (99%)
    pallas_call x1, Pallas kernels, local(): pl.pallas_call(functools.partial(gather_kernel, plan, 2 * mc, mc), out_sh...  29.2 us
    pallas_call x1, Pallas kernels, local(): pl.pallas_call(functools.partial(reduce_kernel, plan, n), out_shape=(sdt(...  26.6 us
    pallas_call x1, Pallas kernels, local(): pl.pallas_call(functools.partial(compute_kernel, plan, mr, mc, gw), out_s...  11.1 us
    pallas_call x1, Pallas kernels, local(): pl.pallas_call(functools.partial(update_kernel, plan), out_shape=(sdt((nc...  1.92 us

profile of v1, /device:TPU:0, one launch (start us, length us, event | category | flops | bytes accessed | tf_op | source)
XLA Modules:
  0.0 69.4 jit_solution(10897553050379197283)
XLA Ops:
  0.6 29.2 %gather.1 = (bf16[3,16,72,128]{3,2,1,0:T(8,128)(2,1)}, bf16[3,16,48,128]{3,2,1,0:T(8,128)(2,1)}, f32[2,16,128]{2,1,0:T(8,128)}, bf16[128,384]{1,0:T(8,128)(2,1)}, bf16[64,768]{1,0:T(8,128)(2,1)}) custom-call(f32[72,384]{1,0:T(8,128)} %bitcast.15, f32[24,768]{1,0:T(8,128)} %bitcast.18, f32[384]{0:T(512)} %gc_ref.3, f32[768]{0:T(1024)} %gp_ref.3, ...), custom_call_target="tpu_custom_call" | custom-call | tf_op jit(solution)/shard_map/gather/pallas_call | solution.py:587
  29.8 11.1 %compute.1 = (bf16[512,384]{1,0:T(8,128)(2,1)}, bf16[3,16,72,128]{3,2,1,0:T(8,128)(2,1)}, bf16[3,16,48,128]{3,2,1,0:T(8,128)(2,1)}) custom-call(bf16[512,384]{1,0:T(8,128)(2,1)} %bitcast.14, bf16[512,768]{1,0:T(8,128)(2,1)} %bitcast.12, bf16[128,384]{1,0:T(8,128)(2,1)} %get-tuple-element.20.hx_ref, bf16[64,768]{1,0:T(8,128)(2,1)} %get-tuple-element.21.hu_ref, ...), custom_call_target="tpu_custom_call" | custom-call | tf_op jit(solution)/shard_map/compute/pallas_call | solution.py:602
  40.9 26.6 %reduce.1 = (f32[3,72,128]{2,1,0:T(8,128)}, f32[3,48,128]{2,1,0:T(8,128)}, f32[2,24,128]{2,1,0:T(8,128)}) custom-call(bf16[3,16,72,128]{3,2,1,0:T(8,128)(2,1)} %get-tuple-element.25.pc_ref, bf16[3,16,48,128]{3,2,1,0:T(8,128)(2,1)} %get-tuple-element.26.pq_ref, f32[72,384]{1,0:T(8,128)} %bitcast.16, f32[24,768]{1,0:T(8,128)} %bitcast.19, ...), custom_call_target="tpu_custom_call" | custom-call | tf_op jit(solution)/shard_map/reduce/pallas_call | solution.py:618
  67.5 1.9 %update.1 = (f32[72,384]{1,0:T(8,128)}, f32[24,768]{1,0:T(8,128)}, f32[72,384]{1,0:T(8,128)}, f32[24,768]{1,0:T(8,128)}) custom-call(f32[3,72,128]{2,1,0:T(8,128)} %get-tuple-element.28.gradc_ref, f32[3,48,128]{2,1,0:T(8,128)} %get-tuple-element.29.gradq_ref, f32[2,24,128]{2,1,0:T(8,128)} %get-tuple-element.30.coef_ref, ...), custom_call_target="tpu_custom_call" | custom-call | tf_op jit(solution)/shard_map/update/pallas_call | solution.py:630

commit v2 on v1

v2 whole, which is shorter than its diff:
```python
import functools
import math

import jax
import jax.numpy as jnp
from jax import lax
from jax.experimental import pallas as pl
from jax.experimental.pallas import tpu as pltpu
from jax.sharding import PartitionSpec as P

ws_eps = 0.0001
clip_ratio = 0.05
momentum_rate = 0.9
learn_rate = 1.6
norm_eps = 1e-06

F32 = jnp.float32
BF16 = jnp.bfloat16
MESH = pl.DeviceIdType.MESH
TAPS = 3
C0 = math.sqrt(2.0 / math.pi)
C1 = 0.044715


def gelu_parts(x):
    t = jnp.tanh(C0 * (x + C1 * (x * x * x)))
    half = 0.5 * (1.0 + t)
    slope = half + (0.5 * C0) * x * (1.0 - t * t) * (1.0 + (3.0 * C1) * (x * x))
    return x * half, slope


def dot_nn(a, b):
    return jnp.dot(a, b, preferred_element_type=F32)


def dot_nt(a, b):
    return lax.dot_general(a, b, (((1,), (1,)), ((), ())), preferred_element_type=F32)


def dot_tn(a, b):
    return lax.dot_general(a, b, (((0,), (0,)), ((), ())), preferred_element_type=F32)


LANE = 128


class Plan:
    def __init__(self, n, ch, out, nc, np_):
        nb = n.bit_length() - 1
        assert 2**nb == n and nb >= 1
        self.n, self.nc, self.np_ = n, nc, np_
        self.nz = 2 ** (nb // 2)
        self.nm = n // 2 // self.nz
        self.half = n // 2
        self.ch, self.out = ch, out
        self.nblk = out // ch
        self.pieces = ch // LANE
        cut = self.pieces // 2
        rest = self.pieces - cut
        self.sets = (
            [("q", k) for k in range(cut)] + [("c", k) for k in range(rest)],
            [("q", k) for k in range(cut, self.pieces)] + [("c", k) for k in range(rest, self.pieces)],
        )
        self.tiles = tuple([t for chunk in one for t in self.tiles_of(chunk)] for one in self.sets)
        self.wide = max(len(t) for t in self.tiles)
        assert self.wide <= 5
        self.proj_tiles = tuple(sum(which for which, _ in one) for one in self.tiles)

    def tiles_of(self, chunk):
        kind, k = chunk
        if kind == "c":
            return [(0, k * LANE)]
        return [(1, b * self.ch + k * LANE) for b in range(self.nblk)]

    def count_of(self, which):
        return self.np_ if which else self.nc

    def chunk_rows(self, kind):
        return self.nc if kind == "c" else self.nblk * self.np_

    def slot(self, d):
        return (d % 2 * self.nm + d // 2 % self.nm) * self.nz + d // 2 // self.nm

    def place(self, me):
        return me % 2, me // 2 % self.nm, me // 2 // self.nm

    def batch(self, c, m, z):
        return (z * self.nm + m) * 2 + c


def send(src, dst, sems, at, where):
    return pltpu.make_async_remote_copy(
        src_ref=src, dst_ref=dst, send_sem=sems[0].at[at], recv_sem=sems[1].at[at],
        device_id=where, device_id_type=MESH,
    )


def greet(plan):
    me = lax.axis_index("batch")
    r = lax.axis_index("rows")
    c, m, z = plan.place(me)
    n = plan.n
    barrier = pltpu.get_barrier_semaphore()
    for d in range(1, n):
        pl.semaphore_signal(barrier, inc=1, device_id={"batch": (me + d) % n}, device_id_type=MESH)
    for j in range(plan.nm):
        to = plan.batch(c, (m + j) % plan.nm, z)
        pl.semaphore_signal(barrier, inc=1, device_id={"batch": to, "rows": 1 - r}, device_id_type=MESH)


def greet_wait(plan):
    pl.semaphore_wait(pltpu.get_barrier_semaphore(), plan.n - 1 + plan.nm)


def push_all(plan, me, src, slots, sems):
    n = plan.n
    copies = []
    for d in range(1, n):
        copy = send(src, slots.at[me], sems, d - 1, {"batch": (me + d) % n})
        copy.start()
        copies.append(copy)
    slots[me] = src[...]
    return copies


def counts_of(plan, r):
    row = lax.broadcasted_iota(jnp.int32, (8, LANE), 0)
    first = jnp.where(r == 0, plan.proj_tiles[0], plan.proj_tiles[1])
    return jnp.where(row < first, float(plan.np_), float(plan.nc))


def merged(plan, slots, cnt):
    w = plan.wide
    total = slots[0]
    for i in range(1, plan.n):
        total = total + slots[i]
    mean = total[0:8] / (plan.n * cnt)
    between = None
    for i in range(plan.n):
        off = slots[i, 0:8] / cnt - mean
        term = cnt * (off * off)
        between = term if between is None else between + term
    return total, mean[0:w], total[w : 2 * w] + between[0:w]


def by_half(r, fn):
    for rr in range(2):
        @pl.when(r == rr)
        def _(rr=rr):
            fn(rr)


def shifted(vals, step, mc):
    rows = vals.shape[0]
    col = lax.broadcasted_iota(jnp.int32, vals.shape, 0)
    if step > 0:
        return jnp.where(col == mc - 1, 0.0, pltpu.roll(vals, rows - 1, 0))
    return jnp.where(col == 0, 0.0, pltpu.roll(vals, 1, 0))


class Refs:
    pass


def main_kernel(plan, names, mr, mc, gw, images, *refs):
    t = Refs()
    for name, ref in zip(names, refs, strict=True):
        setattr(t, name, ref)
    me = lax.axis_index("batch")
    r = lax.axis_index("rows")
    c, m, z = plan.place(me)
    n, nz, nm, w, half = plan.n, plan.nz, plan.nm, plan.wide, plan.half
    nc, np_, nblk, ch = plan.nc, plan.np_, plan.nblk, plan.ch
    groups = ch // gw
    wide = TAPS * gw
    px = mr * mc
    w_refs = (t.wc, t.wp)
    gain_refs = (t.gc, t.gp)
    full = {"c": t.fc, "q": t.fq}
    load_x = pltpu.make_async_copy(t.x_any, t.x, t.load.at[0])
    load_u = pltpu.make_async_copy(t.u_any, t.u, t.load.at[1])
    load_x.start()
    load_u.start()
    greet(plan)

    t.src[...] = jnp.zeros_like(t.src)

    def weight_stats(rr):
        for i, (which, col) in enumerate(plan.tiles[rr]):
            piece = w_refs[which][:, col : col + LANE]
            s = jnp.sum(piece, axis=0, keepdims=True)
            cent = piece - s / piece.shape[0]
            t.src[i : i + 1] = s
            t.src[w + i : w + i + 1] = jnp.sum(cent * cent, axis=0, keepdims=True)

    by_half(r, weight_stats)
    greet_wait(plan)
    push = push_all(plan, me, t.src, t.slots, (t.s_send, t.s_recv))
    halos = []
    for at, (load, ref, out) in enumerate(((load_x, t.x, t.hx), (load_u, t.u, t.hu))):
        load.wait()
        width = out.shape[0]
        first = (1 - r) * (ref.shape[0] - width)
        copy = send(ref.at[pl.ds(first, width)], out, (t.h_send, t.h_recv), at, {"rows": 1 - r})
        copy.start()
        halos.append(copy)

    def place(at, vals):
        act = gelu_parts(vals)[0].astype(BF16).astype(F32)
        for j in range(TAPS):
            moved = act if j == 1 else shifted(act, j - 1, mc)
            moved = moved.astype(BF16)
            for g in range(groups):
                t.xs[pl.ds(at, mc), g * wide + j * gw : g * wide + (j + 1) * gw] = moved[
                    :, g * gw : (g + 1) * gw
                ]

    def body(row, carry):
        at = pl.multiple_of(row * mc, mc)
        place(pl.multiple_of(at + 2 * mc, mc), t.x[pl.ds(at, mc)].astype(F32))
        return carry

    lax.fori_loop(0, mr, body, 0)

    for copy in push:
        copy.wait()
    cnt = counts_of(plan, r)
    _, mean, spread = merged(plan, t.slots, cnt)
    t.stat[r] = jnp.zeros_like(t.stat[0])
    t.stat[r, 0:w] = mean
    t.stat[r, 8 : 8 + w] = spread
    copy = send(t.stat.at[r], t.stat.at[r], (t.h_send, t.h_recv), 2, {"rows": 1 - r})
    copy.start()
    halos.append(copy)
    factor = lax.rsqrt(spread + ws_eps)
    slot = (c * nm + m) * nz + z
    base = (c * nm + m) * nz

    def z_copy(k, j, chunk):
        kind, g = chunk
        at = full[kind].at[g, slot]
        return send(at, at, (t.z_send, t.z_recv), (k, j - 1), {"batch": plan.batch(c, m, (z + j) % nz)})

    def start_z(rr):
        i = 0
        for k, chunk in enumerate(plan.sets[rr]):
            kind, g = chunk
            for b, (which, col) in enumerate(plan.tiles_of(chunk)):
                count = plan.count_of(which)
                scale = gain_refs[which][col : col + LANE][None] * factor[i : i + 1]
                std = (scale * (w_refs[which][:, col : col + LANE] - mean[i : i + 1])).astype(BF16)
                full[kind][g, slot, b * count : (b + 1) * count] = std
                i += 1
            for j in range(1, nz):
                z_copy(k, j, chunk).start()

    by_half(r, start_z)

    def m_copy(k, j, jx, chunk):
        kind, g = chunk
        at = full[kind].at[g, pl.ds(base, nz)]
        where = {"batch": plan.batch(c, (m + j) % nm, z), "rows": (r + jx) % 2}
        return send(at, at, (t.m_send, t.m_recv), (k, jx * nm + j - 1), where)

    peers = [(j, jx) for jx in (1, 0) for j in reversed(range(nm)) if (j, jx) != (0, 0)]

    def spread_m(k):
        def fn(rr):
            chunk = plan.sets[rr][k]
            for j in range(1, nz):
                z_copy(k, j, chunk).wait()
            for j, jx in peers:
                m_copy(k, j, jx, chunk).start()
        by_half(r, fn)

    def finish_m(k):
        def fn(rr):
            for j, jx in peers:
                m_copy(k, j, jx, plan.sets[rr][k]).wait_send()
                m_copy(k, j, jx, plan.sets[(rr + jx) % 2][k]).wait_recv()
        by_half(r, fn)
        for side in range(2):
            d_copy(k, side).start()

    def d_copy(k, side):
        kind, g = plan.sets[side][k]
        at = full[kind].at[g, pl.ds(c * half, half)]
        return send(at, at, (t.d_send, t.d_recv), (k, side), {"batch": plan.batch(1 - c, m, z)})

    def unpack(chunk):
        kind, g = chunk
        lanes = slice(g * LANE, (g + 1) * LANE)
        for d in range(n):
            if kind == "c":
                t.kt[d * nc : (d + 1) * nc, lanes] = t.fc[g, plan.slot(d)]
                continue
            for b in range(nblk):
                t.pt[d * np_ : (d + 1) * np_, b * ch + g * LANE : b * ch + (g + 1) * LANE] = t.fq[
                    g, plan.slot(d), b * np_ : (b + 1) * np_
                ]

    def forward(g, e, up):
        rows = up.shape[0]
        hg = dot_nt(up, t.pt[g * gw : (g + 1) * gw])
        acc = None
        for i in range(TAPS):
            term = dot_nn(
                t.xs[pl.ds(pl.multiple_of((e + i) * mc, mc), rows), g * wide : (g + 1) * wide],
                t.kt[i * wide : (i + 1) * wide, g * gw : (g + 1) * gw],
            )
            acc = term if acc is None else acc + term
        h, slope = gelu_parts(acc)
        t.hid[pl.ds(pl.multiple_of(e * mc, mc), rows), g * gw : (g + 1) * gw] = h.astype(BF16)
        grad = (hg * slope).astype(BF16).astype(F32)
        for q in range(rows // mc):
            here = grad[q * mc : (q + 1) * mc]
            for j in range(TAPS):
                moved = here if j == 1 else shifted(here, 1 - j, mc)
                t.ys[pl.ds(pl.multiple_of((e + q) * mc, mc), mc), g * wide + j * gw : g * wide + (j + 1) * gw] = moved.astype(BF16)

    many = next(k for k in (4, 2, 1) if mr % k == 0)

    def forward_all(g):
        forward(g, jnp.where(r == 1, 0, mr + 1), t.hu[...])

        def fwd(s, carry):
            up = t.u[pl.ds(pl.multiple_of(s * many * mc, mc), many * mc)]
            forward(g, 1 + s * many, up)
            return carry

        lax.fori_loop(0, mr // many, fwd, 0)

    halos[0].wait()
    near = pl.multiple_of(jnp.where(r == 1, 0, (mr + 2) * mc), mc)
    far = pl.multiple_of(jnp.where(r == 1, (mr + 2) * mc, 0), mc)
    t.xs[pl.ds(far, 2 * mc)] = jnp.zeros((2 * mc, t.xs.shape[1]), BF16)
    for e in range(2):
        place(pl.multiple_of(near + e * mc, mc), t.hx[e * mc : (e + 1) * mc].astype(F32))
    outside = pl.multiple_of(jnp.where(r == 1, (mr + 1) * mc, 0), mc)
    t.ys[pl.ds(outside, mc)] = jnp.zeros((mc, t.ys.shape[1]), BF16)
    halos[1].wait()

    for k in range(plan.pieces):
        spread_m(k)
    filled, ran = [], []
    for k in range(plan.pieces):
        finish_m(k)
        if k == 0:
            continue
        upto = k + 1 if k == plan.pieces - 1 else k
        for q in range(k - 1, upto):
            for side in range(2):
                d_copy(q, side).wait()
                unpack(plan.sets[side][q])
                filled.append(plan.sets[side][q])
            if sum(kind == "q" for kind, _ in filled) == plan.pieces:
                for kind, g in filled:
                    if kind == "c" and g not in ran:
                        forward_all(g)
                        ran.append(g)
    assert len(ran) == groups

    part = {"c": t.pc, "q": t.pq}
    got_d = {"c": t.gdc, "q": t.gdq}
    two = {"c": t.twoc, "q": t.twoq}
    got_m = {"c": t.gmc, "q": t.gmq}
    eight = {"c": t.eightc, "q": t.eightq}
    got_z = {"c": t.gzc, "q": t.gzq}
    grads = {"c": t.gradc, "q": t.gradq}

    def produce(chunk):
        kind, g = chunk
        if kind == "c":
            own = t.ys[mc : mc + px, g * wide + gw : g * wide + 2 * gw]
            for i in range(TAPS):
                t.cg[i * wide : (i + 1) * wide] = dot_tn(
                    t.xs[(1 + i) * mc : (1 + i) * mc + px, g * wide : (g + 1) * wide], own
                )
            for d in range(n):
                t.pc[g, plan.slot(d)] = t.cg[d * nc : (d + 1) * nc].astype(BF16)
            return
        for b in range(nblk):
            at = b * ch + g * LANE
            t.pg[:, b * LANE : (b + 1) * LANE] = dot_tn(t.hid[mc : mc + px], t.u[:, at : at + LANE])
        for d in range(n):
            for b in range(nblk):
                t.pq[g, plan.slot(d), b * np_ : (b + 1) * np_] = t.pg[
                    d * np_ : (d + 1) * np_, b * LANE : (b + 1) * LANE
                ].astype(BF16)

    def rd_copy(k, side):
        kind, g = plan.sets[side][k]
        return send(
            part[kind].at[g, pl.ds((1 - c) * half, half)], got_d[kind].at[g],
            (t.rd_send, t.rd_recv), (k, side), {"batch": plan.batch(1 - c, m, z)},
        )

    def rm_copy(k, j, jx, chunk):
        kind, g = chunk
        to = (m + j) % nm
        return send(
            two[kind].at[g, pl.ds(to * nz, nz)], got_m[kind].at[g, jx * nm + j - 1],
            (t.rm_send, t.rm_recv), (k, jx * nm + j - 1),
            {"batch": plan.batch(c, to, z), "rows": (r + jx) % 2},
        )

    def step_m(k):
        for side in range(2):
            rd_copy(k, side).wait()

        def fn(rr):
            for j, jx in peers:
                kind, g = plan.sets[(rr + jx) % 2][k]
                first = (m + j) % nm * nz
                two[kind][g, pl.ds(first, nz)] = (
                    part[kind][g, pl.ds(c * half + first, nz)] + got_d[kind][g, pl.ds(first, nz)]
                )
                rm_copy(k, j, jx, (kind, g)).start()
        by_half(r, fn)

    def rz_copy(k, j, chunk):
        kind, g = chunk
        to = (z + j) % nz
        return send(
            eight[kind].at[g, to], got_z[kind].at[g, j - 1],
            (t.rz_send, t.rz_recv), (k, j - 1), {"batch": plan.batch(c, m, to)},
        )

    def sum_m(kind, g, at):
        first = m * nz + at
        total = part[kind][g, c * half + first].astype(F32) + got_d[kind][g, first].astype(F32)
        for i in range(2 * nm - 1):
            total = total + got_m[kind][g, i, at].astype(F32)
        return total

    def step_z(k):
        def fn(rr):
            for j, jx in peers:
                rm_copy(k, j, jx, plan.sets[(rr + jx) % 2][k]).wait_send()
                rm_copy(k, j, jx, plan.sets[rr][k]).wait_recv()
            kind, g = plan.sets[rr][k]
            for j in range(1, nz):
                to = (z + j) % nz
                eight[kind][g, to] = sum_m(kind, g, to).astype(BF16)
                rz_copy(k, j, (kind, g)).start()
            grads[kind][g] = sum_m(kind, g, z)
        by_half(r, fn)

    def x_copy(k, chunk):
        kind, g = chunk
        return send(grads[kind].at[g], grads[kind].at[g], (t.x_send, t.x_recv), k, {"rows": 1 - r})

    def finish(k):
        def fn(rr):
            kind, g = plan.sets[rr][k]
            total = grads[kind][g]
            for j in range(1, nz):
                rz_copy(k, j, (kind, g)).wait()
                total = total + got_z[kind][g, j - 1].astype(F32)
            grads[kind][g] = total / images
            x_copy(k, (kind, g)).start()
        by_half(r, fn)

    order = list(reversed(range(plan.pieces)))
    before = None
    for k in order:
        for side in range(2):
            produce(plan.sets[side][k])
            rd_copy(k, side).start()
        if before is not None:
            step_m(before)
        before = k
    step_m(before)

    tall = next(k for k in (2, 1) if mr % k == 0)

    def back(s, carry):
        at = pl.multiple_of(s * tall * mc, mc)
        for g in range(groups):
            acc = None
            for i in range(TAPS):
                for j in range(TAPS):
                    term = dot_nt(
                        t.ys[pl.ds(pl.multiple_of(at + (2 - i) * mc, mc), tall * mc), g * wide + j * gw : g * wide + (j + 1) * gw],
                        t.kt[i * wide + j * gw : i * wide + (j + 1) * gw, g * gw : (g + 1) * gw],
                    )
                    acc = term if acc is None else acc + term
            slope = gelu_parts(t.x[pl.ds(at, tall * mc), g * gw : (g + 1) * gw].astype(F32))[1]
            t.ig[pl.ds(at, tall * mc), g * gw : (g + 1) * gw] = (acc * slope).astype(BF16)
        return carry

    lax.fori_loop(0, mr // tall, back, 0)
    store = pltpu.make_async_copy(t.ig, t.ig_any, t.load.at[2])
    store.start()
    for k in order:
        step_z(k)
    for k in order:
        finish(k)

    t.src[...] = jnp.zeros_like(t.src)
    t.gain[...] = jnp.zeros_like(t.gain)

    def grad_stats(rr):
        i = 0
        for chunk in plan.sets[rr]:
            kind, g = chunk
            for b, (which, col) in enumerate(plan.tiles_of(chunk)):
                count = plan.count_of(which)
                piece = grads[kind][g, b * count : (b + 1) * count]
                cent = w_refs[which][:, col : col + LANE] - t.stat[rr, i : i + 1]
                s = jnp.sum(piece, axis=0, keepdims=True)
                off = piece - s / count
                t.src[i : i + 1] = s
                t.src[w + i : w + i + 1] = jnp.sum(off * off, axis=0, keepdims=True)
                t.src[2 * w + i : 2 * w + i + 1] = jnp.sum(piece * cent, axis=0, keepdims=True)
                t.gain[i : i + 1] = gain_refs[which][col : col + LANE][None]
                i += 1

    by_half(r, grad_stats)
    for copy in push_all(plan, me, t.src, t.slots2, (t.s2_send, t.s2_recv)):
        copy.wait()
    total, gmean, gspread = merged(plan, t.slots2, cnt)
    proj = total[2 * w : 3 * w]
    fan = n * cnt[0:w]
    mean = t.stat[r, 0:w]
    spread = t.stat[r, 8 : 8 + w]
    factor = lax.rsqrt(spread + ws_eps)
    f2 = factor * factor
    one = t.gain[0:w] * factor
    coef_two = one * f2 * proj
    grad_sq = one * one * jnp.maximum(gspread - f2 * proj * proj * (2.0 - f2 * spread), 0.0)
    weight_sq = spread + fan * (mean * mean)
    clip = jnp.minimum(1.0, clip_ratio * jnp.sqrt(weight_sq) * lax.rsqrt(grad_sq + norm_eps))
    t.coef[r] = jnp.zeros_like(t.coef[0])
    t.coef[r, 0:w] = clip * one
    t.coef[r, 8 : 8 + w] = gmean
    t.coef[r, 16 : 16 + w] = clip * coef_two
    last = send(t.coef.at[r], t.coef.at[r], (t.x_send, t.x_recv), plan.pieces, {"rows": 1 - r})
    last.start()

    def end(rr):
        for k in range(plan.pieces):
            x_copy(k, plan.sets[rr][k]).wait_send()
            x_copy(k, plan.sets[1 - rr][k]).wait_recv()

    by_half(r, end)
    halos[2].wait()
    store.wait()
    last.wait()


def update_kernel(plan, gradc_ref, gradq_ref, coef_ref, stat_ref, wc_ref, wp_ref, mc_ref, mp_ref, ig_in,
                  nwc_ref, nwp_ref, nmc_ref, nmp_ref, ig_out, ig, sems):
    fetch = pltpu.make_async_copy(ig_in, ig, sems.at[0])
    store = pltpu.make_async_copy(ig, ig_out, sems.at[1])
    fetch.start()
    fetch.wait()
    store.start()
    grads = {"c": gradc_ref, "q": gradq_ref}
    for rr in range(2):
        i = 0
        for chunk in plan.sets[rr]:
            kind, g = chunk
            for b, (which, col) in enumerate(plan.tiles_of(chunk)):
                count = plan.count_of(which)
                cols = slice(col, col + LANE)
                w = (wc_ref, wp_ref)[which][:, cols]
                grad = grads[kind][g, b * count : (b + 1) * count]
                clipped = coef_ref[rr, i : i + 1] * (grad - coef_ref[rr, 8 + i : 9 + i]) - coef_ref[
                    rr, 16 + i : 17 + i
                ] * (w - stat_ref[rr, i : i + 1])
                new_m = momentum_rate * (mc_ref, mp_ref)[which][:, cols] + clipped
                (nmc_ref, nmp_ref)[which][:, cols] = new_m
                (nwc_ref, nwp_ref)[which][:, cols] = w - learn_rate * (clipped + momentum_rate * new_m)
                i += 1
    store.wait()


def local(n, nrows, block_input, output_grad, conv_weight, conv_gain, conv_momentum,
          proj_weight, proj_gain, proj_momentum):
    assert nrows == 2
    _, mr, mc, ch = block_input.shape
    out = output_grad.shape[3]
    nc = conv_weight.shape[1]
    np_ = proj_weight.shape[1]
    gw = nc * n // (TAPS * TAPS)
    assert gw == LANE
    plan = Plan(n, ch, out, nc, np_)
    nz, nm, half, pieces = plan.nz, plan.nm, plan.half, plan.pieces
    px = mr * mc
    rq = plan.chunk_rows("q")

    wc, wp, mc_, mp = conv_weight.T, proj_weight.T, conv_momentum.T, proj_momentum.T
    gc, gp = conv_gain, proj_gain
    x = block_input.reshape(px, ch)
    u = output_grad.reshape(px, out)
    vmem = pl.BlockSpec(memory_space=pltpu.VMEM)
    anym = pl.BlockSpec(memory_space=pl.ANY)
    sdt = jax.ShapeDtypeStruct
    dma = pltpu.SemaphoreType.DMA
    scratch = {}

    def pair(name, shape):
        scratch[name + "_send"] = dma(shape)
        scratch[name + "_recv"] = dma(shape)

    def both(name, *lead):
        scratch[name + "c"] = pltpu.VMEM((pieces, *lead, nc, LANE), BF16)
        scratch[name + "q"] = pltpu.VMEM((pieces, *lead, rq, LANE), BF16)

    scratch.update(
        x=pltpu.VMEM((px, ch), BF16),
        u=pltpu.VMEM((px, out), BF16),
        ig=pltpu.VMEM((px, ch), BF16),
        hx=pltpu.VMEM((2 * mc, ch), BF16),
        hu=pltpu.VMEM((mc, out), BF16),
        kt=pltpu.VMEM((n * nc, ch), BF16),
        pt=pltpu.VMEM((n * np_, out), BF16),
        xs=pltpu.VMEM(((mr + 4) * mc, TAPS * ch), BF16),
        ys=pltpu.VMEM(((mr + 2) * mc, TAPS * ch), BF16),
        hid=pltpu.VMEM(((mr + 2) * mc, ch), BF16),
        cg=pltpu.VMEM((n * nc, LANE), F32),
        pg=pltpu.VMEM((n * np_, plan.nblk * LANE), F32),
        src=pltpu.VMEM((16, LANE), F32),
        slots=pltpu.VMEM((n, 16, LANE), F32),
        slots2=pltpu.VMEM((n, 16, LANE), F32),
        gain=pltpu.VMEM((8, LANE), F32),
        load=dma((3,)),
    )
    for name, lead in (("f", (n,)), ("p", (n,)), ("gd", (half,)), ("two", (half,)),
                       ("gm", (2 * nm - 1, nz)), ("eight", (nz,)), ("gz", (max(nz - 1, 1),))):
        both(name, *lead)
    for name in ("s", "s2"):
        pair(name, (n - 1,))
    for name in ("z", "rz"):
        pair(name, (pieces, max(nz - 1, 1)))
    for name in ("m", "rm"):
        pair(name, (pieces, 2 * nm - 1))
    for name in ("d", "rd"):
        pair(name, (pieces, 2))
    pair("h", (3,))
    pair("x", (pieces + 1,))
    names = ["wc", "wp", "gc", "gp", "x_any", "u_any", "ig_any", "gradc", "gradq", "coef", "stat", *scratch]
    ig, gradc, gradq, coef, stat = pl.pallas_call(
        functools.partial(main_kernel, plan, names, mr, mc, gw, n),
        out_shape=(
            sdt((px, ch), BF16),
            sdt((pieces, nc, LANE), F32),
            sdt((pieces, rq, LANE), F32),
            sdt((2, 24, LANE), F32),
            sdt((2, 16, LANE), F32),
        ),
        in_specs=[vmem] * 4 + [anym] * 2,
        out_specs=(anym,) + (vmem,) * 4,
        scratch_shapes=list(scratch.values()),
        compiler_params=pltpu.CompilerParams(collective_id=0, has_side_effects=True),
        name="main",
    )(wc, wp, gc, gp, x, u)
    nwc, nwp, nmc, nmp, ig = pl.pallas_call(
        functools.partial(update_kernel, plan),
        out_shape=(sdt((nc, ch), F32), sdt((np_, out), F32)) * 2 + (sdt((px, ch), BF16),),
        in_specs=[vmem] * 8 + [anym],
        out_specs=(vmem,) * 4 + (anym,),
        scratch_shapes=[pltpu.VMEM((px, ch), BF16), dma((2,))],
        name="update",
    )(gradc, gradq, coef, stat, wc, wp, mc_, mp, ig)
    return (ig.reshape(block_input.shape), nwc.T, nmc.T, nwp.T, nmp.T)


def solution(mesh):
    in_specs = (
        P("batch", "rows", None, None),
        P("batch", "rows", None, None),
        P(None, "batch"),
        P(),
        P(None, "batch"),
        P(None, "batch"),
        P(),
        P(None, "batch"),
    )
    out_specs = (
        P("batch", "rows", None, None),
        P(None, "batch"),
        P(None, "batch"),
        P(None, "batch"),
        P(None, "batch"),
    )
    body = functools.partial(local, mesh.shape["batch"], mesh.shape["rows"])
    return jax.shard_map(body, mesh=mesh, in_specs=in_specs, out_specs=out_specs, check_vma=False)
```

time: 69.7 us -> 58.7 us (0.84)
  Pallas kernels: 68.8 us -> 57.9 us
    pallas_call x3 -> x1, Pallas kernels: 66.9 us -> 54.2 us  [local(): pl.pallas_call(functools.partial(main_kernel, plan, names, mr, mc, gw, n)...]
    pallas_call x1, Pallas kernels: 1.92 us -> 3.64 us  [local(): pl.pallas_call(functools.partial(update_kernel, plan), out_shape=(sdt((nc...]
where the time goes in v2:
time: 58.7 us; the launch traced here: 58.5 us
  Pallas kernels  57.9 us (99%)
  between operations  0.64 us (1%)
    pallas_call x1, Pallas kernels, local(): pl.pallas_call(functools.partial(main_kernel, plan, names, mr, mc, gw, n)...  54.2 us
    pallas_call x1, Pallas kernels, local(): pl.pallas_call(functools.partial(update_kernel, plan), out_shape=(sdt((nc...  3.64 us

profile of v2, /device:TPU:0, one launch (start us, length us, event | category | flops | bytes accessed | tf_op | source)
XLA Modules:
  0.0 58.5 jit_solution(6662583886786266752)
XLA Ops:
  0.6 54.2 %main.1 = (bf16[512,384]{1,0:T(8,128)(2,1)}, f32[3,72,128]{2,1,0:T(8,128)}, f32[3,48,128]{2,1,0:T(8,128)}, f32[2,24,128]{2,1,0:T(8,128)}, f32[2,16,128]{2,1,0:T(8,128)}) custom-call(f32[72,384]{1,0:T(8,128)} %bitcast.12, f32[24,768]{1,0:T(8,128)} %bitcast.15, f32[384]{0:T(512)} %refs_2_.1, f32[768]{0:T(1024)} %refs_3_.1, bf16[512,384]{1,0:T(8,128)(2,1)} %bitcast.14, ...), custom_call_target="tpu_custom_call" | custom-call | tf_op jit(solution)/shard_map/main/pallas_call | solution.py:644
  54.9 3.6 %update.1 = (f32[72,384]{1,0:T(8,128)}, f32[24,768]{1,0:T(8,128)}, f32[72,384]{1,0:T(8,128)}, f32[24,768]{1,0:T(8,128)}, bf16[512,384]{1,0:T(8,128)(2,1)}) custom-call(f32[3,72,128]{2,1,0:T(8,128)} %get-tuple-element.15.gradc_ref, f32[3,48,128]{2,1,0:T(8,128)} %get-tuple-element.16.gradq_ref, f32[2,24,128]{2,1,0:T(8,128)} %get-tuple-element.17.coef_ref, ...), custom_call_target="tpu_custom_call" | custom-call | tf_op jit(solution)/shard_map/update/pallas_call | solution.py:659

commit v3 on v2

--- a/solution.py
+++ b/solution.py
@@ -62,9 +62,12 @@
             [("q", k) for k in range(cut, self.pieces)] + [("c", k) for k in range(rest, self.pieces)],
         )
         self.tiles = tuple([t for chunk in one for t in self.tiles_of(chunk)] for one in self.sets)
+        self.lead = self.nblk
         self.wide = max(len(t) for t in self.tiles)
-        assert self.wide <= 5
-        self.proj_tiles = tuple(sum(which for which, _ in one) for one in self.tiles)
+        assert cut and self.wide <= 8 and self.wide - self.lead <= 4
+        self.starts = tuple(
+            [sum(len(self.tiles_of(chunk)) for chunk in one[:k]) for k in range(self.pieces)] for one in self.sets
+        )
 
     def tiles_of(self, chunk):
         kind, k = chunk
@@ -98,49 +101,30 @@
 def greet(plan):
     me = lax.axis_index("batch")
     r = lax.axis_index("rows")
-    c, m, z = plan.place(me)
     n = plan.n
     barrier = pltpu.get_barrier_semaphore()
     for d in range(1, n):
         pl.semaphore_signal(barrier, inc=1, device_id={"batch": (me + d) % n}, device_id_type=MESH)
-    for j in range(plan.nm):
-        to = plan.batch(c, (m + j) % plan.nm, z)
+    for d in range(plan.half):
+        to = (me + 2 * d) % n
         pl.semaphore_signal(barrier, inc=1, device_id={"batch": to, "rows": 1 - r}, device_id_type=MESH)
 
 
 def greet_wait(plan):
-    pl.semaphore_wait(pltpu.get_barrier_semaphore(), plan.n - 1 + plan.nm)
-
-
-def push_all(plan, me, src, slots, sems):
-    n = plan.n
-    copies = []
-    for d in range(1, n):
-        copy = send(src, slots.at[me], sems, d - 1, {"batch": (me + d) % n})
-        copy.start()
-        copies.append(copy)
-    slots[me] = src[...]
-    return copies
-
-
-def counts_of(plan, r):
-    row = lax.broadcasted_iota(jnp.int32, (8, LANE), 0)
-    first = jnp.where(r == 0, plan.proj_tiles[0], plan.proj_tiles[1])
-    return jnp.where(row < first, float(plan.np_), float(plan.nc))
-
-
-def merged(plan, slots, cnt):
-    w = plan.wide
-    total = slots[0]
-    for i in range(1, plan.n):
-        total = total + slots[i]
-    mean = total[0:8] / (plan.n * cnt)
+    pl.semaphore_wait(pltpu.get_barrier_semaphore(), plan.n - 1 + plan.half)
+
+
+def merged(entries, cnt):
+    total = entries[0]
+    for one in entries[1:]:
+        total = total + one
+    mean = total / (len(entries) * cnt)
     between = None
-    for i in range(plan.n):
-        off = slots[i, 0:8] / cnt - mean
+    for one in entries:
+        off = one / cnt - mean
         term = cnt * (off * off)
         between = term if between is None else between + term
-    return total, mean[0:w], total[w : 2 * w] + between[0:w]
+    return total, mean, between
 
 
 def by_half(r, fn):
@@ -169,7 +153,7 @@
     me = lax.axis_index("batch")
     r = lax.axis_index("rows")
     c, m, z = plan.place(me)
-    n, nz, nm, w, half = plan.n, plan.nz, plan.nm, plan.wide, plan.half
+    n, nz, nm, half = plan.n, plan.nz, plan.nm, plan.half
     nc, np_, nblk, ch = plan.nc, plan.np_, plan.nblk, plan.ch
     groups = ch // gw
     wide = TAPS * gw
@@ -177,10 +161,12 @@
     w_refs = (t.wc, t.wp)
     gain_refs = (t.gc, t.gp)
     full = {"c": t.fc, "q": t.fq}
-    load_x = pltpu.make_async_copy(t.x_any, t.x, t.load.at[0])
-    load_u = pltpu.make_async_copy(t.u_any, t.u, t.load.at[1])
-    load_x.start()
-    load_u.start()
+    loads = []
+    for at, (far, near) in enumerate(((t.wc_any, t.wc), (t.wp_any, t.wp), (t.gc_any, t.gc), (t.gp_any, t.gp),
+                                      (t.x_any, t.x), (t.u_any, t.u))):
+        copy = pltpu.make_async_copy(far, near, t.load.at[at])
+        copy.start()
+        loads.append(copy)
     greet(plan)
 
     t.src[...] = jnp.zeros_like(t.src)
@@ -190,14 +176,26 @@
             piece = w_refs[which][:, col : col + LANE]
             s = jnp.sum(piece, axis=0, keepdims=True)
             cent = piece - s / piece.shape[0]
-            t.src[i : i + 1] = s
-            t.src[w + i : w + i + 1] = jnp.sum(cent * cent, axis=0, keepdims=True)
-
+            late = int(i >= plan.lead)
+            row = i - late * plan.lead
+            t.src[late, row : row + 1] = s
+            t.src[late, 4 + row : 5 + row] = jnp.sum(cent * cent, axis=0, keepdims=True)
+
+    for copy in loads[:4]:
+        copy.wait()
     by_half(r, weight_stats)
     greet_wait(plan)
-    push = push_all(plan, me, t.src, t.slots, (t.s_send, t.s_recv))
+    push = [[], []]
+    for late in range(2):
+        for d in range(1, n):
+            copy = send(
+                t.src.at[late], t.slots.at[late, me], (t.s_send, t.s_recv), (late, d - 1), {"batch": (me + d) % n}
+            )
+            copy.start()
+            push[late].append(copy)
+        t.slots[late, me] = t.src[late]
     halos = []
-    for at, (load, ref, out) in enumerate(((load_x, t.x, t.hx), (load_u, t.u, t.hu))):
+    for at, (load, ref, out) in enumerate(((loads[4], t.x, t.hx), (loads[5], t.u, t.hu))):
         load.wait()
         width = out.shape[0]
         first = (1 - r) * (ref.shape[0] - width)
@@ -221,18 +219,11 @@
         return carry
 
     lax.fori_loop(0, mr, body, 0)
-
-    for copy in push:
-        copy.wait()
-    cnt = counts_of(plan, r)
-    _, mean, spread = merged(plan, t.slots, cnt)
-    t.stat[r] = jnp.zeros_like(t.stat[0])
-    t.stat[r, 0:w] = mean
-    t.stat[r, 8 : 8 + w] = spread
-    copy = send(t.stat.at[r], t.stat.at[r], (t.h_send, t.h_recv), 2, {"rows": 1 - r})
-    copy.start()
-    halos.append(copy)
-    factor = lax.rsqrt(spread + ws_eps)
+    t.gain[...] = jnp.zeros_like(t.gain)
+    for rr in range(2):
+        for i, (which, col) in enumerate(plan.tiles[rr]):
+            t.gain[rr, i : i + 1] = gain_refs[which][col : col + LANE][None]
+
     slot = (c * nm + m) * nz + z
     base = (c * nm + m) * nz
 
@@ -241,20 +232,40 @@
         at = full[kind].at[g, slot]
         return send(at, at, (t.z_send, t.z_recv), (k, j - 1), {"batch": plan.batch(c, m, (z + j) % nz)})
 
-    def start_z(rr):
-        i = 0
-        for k, chunk in enumerate(plan.sets[rr]):
-            kind, g = chunk
-            for b, (which, col) in enumerate(plan.tiles_of(chunk)):
-                count = plan.count_of(which)
-                scale = gain_refs[which][col : col + LANE][None] * factor[i : i + 1]
-                std = (scale * (w_refs[which][:, col : col + LANE] - mean[i : i + 1])).astype(BF16)
-                full[kind][g, slot, b * count : (b + 1) * count] = std
-                i += 1
-            for j in range(1, nz):
-                z_copy(k, j, chunk).start()
-
-    by_half(r, start_z)
+    t.stat[r] = jnp.zeros_like(t.stat[0])
+    row = lax.broadcasted_iota(jnp.int32, (8, LANE), 0)
+    for late in range(2):
+        for copy in push[late]:
+            copy.wait()
+        ks = range(1, plan.pieces) if late else range(1)
+        tiles = [plan.tiles[rr][plan.lead :] if late else plan.tiles[rr][: plan.lead] for rr in range(2)]
+        first = [sum(which for which, _ in one) for one in tiles]
+        most = max(len(one) for one in tiles)
+        cnt = jnp.where(row < jnp.where(r == 0, first[0], first[1]), float(np_), float(nc))
+        total, mean, between = merged([t.slots[late, i] for i in range(n)], cnt)
+        spread = total[4 : 4 + most] + between[0:most]
+        factor = lax.rsqrt(spread + ws_eps)
+        at = late * plan.lead
+        t.stat[r, at : at + most] = mean[0:most]
+        t.stat[r, 8 + at : 8 + at + most] = spread
+
+        def start_z(rr, ks=ks, mean=mean, factor=factor):
+            i = 0
+            for k in ks:
+                kind, g = plan.sets[rr][k]
+                for b, (which, col) in enumerate(plan.tiles_of((kind, g))):
+                    count = plan.count_of(which)
+                    scale = gain_refs[which][col : col + LANE][None] * factor[i : i + 1]
+                    std = (scale * (w_refs[which][:, col : col + LANE] - mean[i : i + 1])).astype(BF16)
+                    full[kind][g, slot, b * count : (b + 1) * count] = std
+                    i += 1
+                for j in range(1, nz):
+                    z_copy(k, j, (kind, g)).start()
+
+        by_half(r, start_z)
+    copy = send(t.stat.at[r], t.stat.at[r], (t.h_send, t.h_recv), 2, {"rows": 1 - r})
+    copy.start()
+    halos.append(copy)
 
     def m_copy(k, j, jx, chunk):
         kind, g = chunk
@@ -450,6 +461,12 @@
         kind, g = chunk
         return send(grads[kind].at[g], grads[kind].at[g], (t.x_send, t.x_recv), k, {"rows": 1 - r})
 
+    lead = plan.lead
+    chip = m * nz + z
+
+    def swap(k):
+        return send(t.src2.at[k], t.other.at[k], (t.c_send, t.c_recv), k, {"batch": plan.batch(1 - c, m, z)})
+
     def finish(k):
         def fn(rr):
             kind, g = plan.sets[rr][k]
@@ -457,9 +474,66 @@
             for j in range(1, nz):
                 rz_copy(k, j, (kind, g)).wait()
                 total = total + got_z[kind][g, j - 1].astype(F32)
-            grads[kind][g] = total / images
-            x_copy(k, (kind, g)).start()
+            total = total / images
+            grads[kind][g] = total
+            for b, (which, col) in enumerate(plan.tiles_of((kind, g))):
+                count = plan.count_of(which)
+                i = plan.starts[rr][k] + b
+                piece = total[b * count : (b + 1) * count]
+                cent = w_refs[which][:, col : col + LANE] - t.stat[rr, i : i + 1]
+                s = jnp.sum(piece, axis=0, keepdims=True)
+                off = piece - s / count
+                t.src2[k, b : b + 1] = s
+                t.src2[k, lead + b : lead + b + 1] = jnp.sum(off * off, axis=0, keepdims=True)
+                t.src2[k, 2 * lead + b : 2 * lead + b + 1] = jnp.sum(piece * cent, axis=0, keepdims=True)
+            swap(k).start()
+            if k != order[-1]:
+                x_copy(k, (kind, g)).start()
         by_half(r, fn)
+
+    def count_at(rr, k):
+        return float(plan.nc if plan.sets[rr][k][0] == "c" else plan.np_)
+
+    def stat_copies(k):
+        return [
+            send(
+                t.both.at[k], t.slots2.at[k, r, chip], (t.s2_send, t.s2_recv), (k, jx * half + d - 1),
+                {"batch": (me + 2 * d) % n, "rows": (r + jx) % 2},
+            )
+            for jx in (1, 0) for d in range(half) if (d, jx) != (0, 0)
+        ]
+
+    def share(k):
+        swap(k).wait()
+        total, _, between = merged([t.src2[k], t.other[k]], jnp.where(r == 0, count_at(0, k), count_at(1, k)))
+        t.both[k] = total
+        t.both[k, lead : 2 * lead] = total[lead : 2 * lead] + between[0:lead]
+        for copy in stat_copies(k):
+            copy.start()
+        t.slots2[k, r, chip] = t.both[k]
+
+    def coefs(k):
+        for copy in stat_copies(k):
+            copy.wait()
+        for rr in range(2):
+            count = count_at(rr, k)
+            many = len(plan.tiles_of(plan.sets[rr][k]))
+            at = plan.starts[rr][k]
+            total, gmean, between = merged([t.slots2[k, rr, i] for i in range(half)], 2.0 * count)
+            gspread = total[lead : lead + many] + between[0:many]
+            proj = total[2 * lead : 2 * lead + many]
+            mean = t.stat[rr, at : at + many]
+            spread = t.stat[rr, 8 + at : 8 + at + many]
+            factor = lax.rsqrt(spread + ws_eps)
+            f2 = factor * factor
+            one = t.gain[rr, at : at + many] * factor
+            coef_two = one * f2 * proj
+            grad_sq = one * one * jnp.maximum(gspread - f2 * proj * proj * (2.0 - f2 * spread), 0.0)
+            weight_sq = spread + n * count * (mean * mean)
+            clip = jnp.minimum(1.0, clip_ratio * jnp.sqrt(weight_sq) * lax.rsqrt(grad_sq + norm_eps))
+            t.coef[rr, at : at + many] = clip * one
+            t.coef[rr, 8 + at : 8 + at + many] = gmean[0:many]
+            t.coef[rr, 16 + at : 16 + at + many] = clip * coef_two
 
     order = list(reversed(range(plan.pieces)))
     before = None
@@ -490,53 +564,25 @@
         return carry
 
     lax.fori_loop(0, mr // tall, back, 0)
-    store = pltpu.make_async_copy(t.ig, t.ig_any, t.load.at[2])
-    store.start()
     for k in order:
         step_z(k)
+    t.src2[...] = jnp.zeros_like(t.src2)
+    ahead = []
     for k in order:
         finish(k)
-
-    t.src[...] = jnp.zeros_like(t.src)
-    t.gain[...] = jnp.zeros_like(t.gain)
-
-    def grad_stats(rr):
-        i = 0
-        for chunk in plan.sets[rr]:
-            kind, g = chunk
-            for b, (which, col) in enumerate(plan.tiles_of(chunk)):
-                count = plan.count_of(which)
-                piece = grads[kind][g, b * count : (b + 1) * count]
-                cent = w_refs[which][:, col : col + LANE] - t.stat[rr, i : i + 1]
-                s = jnp.sum(piece, axis=0, keepdims=True)
-                off = piece - s / count
-                t.src[i : i + 1] = s
-                t.src[w + i : w + i + 1] = jnp.sum(off * off, axis=0, keepdims=True)
-                t.src[2 * w + i : 2 * w + i + 1] = jnp.sum(piece * cent, axis=0, keepdims=True)
-                t.gain[i : i + 1] = gain_refs[which][col : col + LANE][None]
-                i += 1
-
-    by_half(r, grad_stats)
-    for copy in push_all(plan, me, t.src, t.slots2, (t.s2_send, t.s2_recv)):
-        copy.wait()
-    total, gmean, gspread = merged(plan, t.slots2, cnt)
-    proj = total[2 * w : 3 * w]
-    fan = n * cnt[0:w]
-    mean = t.stat[r, 0:w]
-    spread = t.stat[r, 8 : 8 + w]
-    factor = lax.rsqrt(spread + ws_eps)
-    f2 = factor * factor
-    one = t.gain[0:w] * factor
-    coef_two = one * f2 * proj
-    grad_sq = one * one * jnp.maximum(gspread - f2 * proj * proj * (2.0 - f2 * spread), 0.0)
-    weight_sq = spread + fan * (mean * mean)
-    clip = jnp.minimum(1.0, clip_ratio * jnp.sqrt(weight_sq) * lax.rsqrt(grad_sq + norm_eps))
-    t.coef[r] = jnp.zeros_like(t.coef[0])
-    t.coef[r, 0:w] = clip * one
-    t.coef[r, 8 : 8 + w] = gmean
-    t.coef[r, 16 : 16 + w] = clip * coef_two
-    last = send(t.coef.at[r], t.coef.at[r], (t.x_send, t.x_recv), plan.pieces, {"rows": 1 - r})
-    last.start()
+        if len(ahead) == 2:
+            share(ahead.pop(0))
+        ahead.append(k)
+    for k in ahead:
+        share(k)
+
+    def last_x(rr):
+        x_copy(order[-1], plan.sets[rr][order[-1]]).start()
+
+    by_half(r, last_x)
+    halos[2].wait()
+    for k in order:
+        coefs(k)
 
     def end(rr):
         for k in range(plan.pieces):
@@ -544,17 +590,11 @@
             x_copy(k, plan.sets[1 - rr][k]).wait_recv()
 
     by_half(r, end)
-    halos[2].wait()
-    store.wait()
-    last.wait()
 
 
 def update_kernel(plan, gradc_ref, gradq_ref, coef_ref, stat_ref, wc_ref, wp_ref, mc_ref, mp_ref, ig_in,
-                  nwc_ref, nwp_ref, nmc_ref, nmp_ref, ig_out, ig, sems):
-    fetch = pltpu.make_async_copy(ig_in, ig, sems.at[0])
-    store = pltpu.make_async_copy(ig, ig_out, sems.at[1])
-    fetch.start()
-    fetch.wait()
+                  nwc_ref, nwp_ref, nmc_ref, nmp_ref, ig_out, sem):
+    store = pltpu.make_async_copy(ig_in, ig_out, sem)
     store.start()
     grads = {"c": gradc_ref, "q": gradq_ref}
     for rr in range(2):
@@ -576,6 +616,10 @@
     store.wait()
 
 
+main_vmem = 40 * 2**20
+update_vmem = 8 * 2**20
+
+
 def local(n, nrows, block_input, output_grad, conv_weight, conv_gain, conv_momentum,
           proj_weight, proj_gain, proj_momentum):
     assert nrows == 2
@@ -594,8 +638,8 @@
     gc, gp = conv_gain, proj_gain
     x = block_input.reshape(px, ch)
     u = output_grad.reshape(px, out)
+    wc, wp, gc, gp, x, u = (pltpu.with_memory_space_constraint(a, pltpu.HBM) for a in (wc, wp, gc, gp, x, u))
     vmem = pl.BlockSpec(memory_space=pltpu.VMEM)
-    anym = pl.BlockSpec(memory_space=pl.ANY)
     sdt = jax.ShapeDtypeStruct
     dma = pltpu.SemaphoreType.DMA
     scratch = {}
@@ -611,7 +655,8 @@
     scratch.update(
         x=pltpu.VMEM((px, ch), BF16),
         u=pltpu.VMEM((px, out), BF16),
-        ig=pltpu.VMEM((px, ch), BF16),
+        gc=pltpu.VMEM((ch,), F32),
+        gp=pltpu.VMEM((out,), F32),
         hx=pltpu.VMEM((2 * mc, ch), BF16),
         hu=pltpu.VMEM((mc, out), BF16),
         kt=pltpu.VMEM((n * nc, ch), BF16),
@@ -621,17 +666,21 @@
         hid=pltpu.VMEM(((mr + 2) * mc, ch), BF16),
         cg=pltpu.VMEM((n * nc, LANE), F32),
         pg=pltpu.VMEM((n * np_, plan.nblk * LANE), F32),
-        src=pltpu.VMEM((16, LANE), F32),
-        slots=pltpu.VMEM((n, 16, LANE), F32),
-        slots2=pltpu.VMEM((n, 16, LANE), F32),
-        gain=pltpu.VMEM((8, LANE), F32),
-        load=dma((3,)),
+        src=pltpu.VMEM((2, 8, LANE), F32),
+        slots=pltpu.VMEM((2, n, 8, LANE), F32),
+        src2=pltpu.VMEM((pieces, 8, LANE), F32),
+        other=pltpu.VMEM((pieces, 8, LANE), F32),
+        both=pltpu.VMEM((pieces, 8, LANE), F32),
+        slots2=pltpu.VMEM((pieces, 2, half, 8, LANE), F32),
+        gain=pltpu.VMEM((2, 8, LANE), F32),
+        load=dma((6,)),
     )
     for name, lead in (("f", (n,)), ("p", (n,)), ("gd", (half,)), ("two", (half,)),
                        ("gm", (2 * nm - 1, nz)), ("eight", (nz,)), ("gz", (max(nz - 1, 1),))):
         both(name, *lead)
-    for name in ("s", "s2"):
-        pair(name, (n - 1,))
+    pair("s", (2, n - 1))
+    pair("s2", (pieces, n - 1))
+    pair("c", (pieces,))
     for name in ("z", "rz"):
         pair(name, (pieces, max(nz - 1, 1)))
     for name in ("m", "rm"):
@@ -640,8 +689,8 @@
         pair(name, (pieces, 2))
     pair("h", (3,))
     pair("x", (pieces + 1,))
-    names = ["wc", "wp", "gc", "gp", "x_any", "u_any", "ig_any", "gradc", "gradq", "coef", "stat", *scratch]
-    ig, gradc, gradq, coef, stat = pl.pallas_call(
+    names = ["wc_any", "wp_any", "gc_any", "gp_any", "x_any", "u_any", "ig", "gradc", "gradq", "coef", "stat", "wc", "wp", *scratch]
+    ig, gradc, gradq, coef, stat, wc, wp = pl.pallas_call(
         functools.partial(main_kernel, plan, names, mr, mc, gw, n),
         out_shape=(
             sdt((px, ch), BF16),
@@ -649,19 +698,24 @@
             sdt((pieces, rq, LANE), F32),
             sdt((2, 24, LANE), F32),
             sdt((2, 16, LANE), F32),
+            sdt((nc, ch), F32),
+            sdt((np_, out), F32),
         ),
-        in_specs=[vmem] * 4 + [anym] * 2,
-        out_specs=(anym,) + (vmem,) * 4,
+        in_specs=[pl.BlockSpec(memory_space=pltpu.HBM)] * 6,
+        out_specs=(vmem,) * 7,
         scratch_shapes=list(scratch.values()),
-        compiler_params=pltpu.CompilerParams(collective_id=0, has_side_effects=True),
+        compiler_params=pltpu.CompilerParams(
+            collective_id=0, has_side_effects=True, vmem_limit_bytes=main_vmem
+        ),
         name="main",
     )(wc, wp, gc, gp, x, u)
     nwc, nwp, nmc, nmp, ig = pl.pallas_call(
         functools.partial(update_kernel, plan),
         out_shape=(sdt((nc, ch), F32), sdt((np_, out), F32)) * 2 + (sdt((px, ch), BF16),),
-        in_specs=[vmem] * 8 + [anym],
-        out_specs=(vmem,) * 4 + (anym,),
-        scratch_shapes=[pltpu.VMEM((px, ch), BF16), dma((2,))],
+        in_specs=[vmem] * 9,
+        out_specs=(vmem,) * 4 + (pl.BlockSpec(memory_space=pl.ANY),),
+        scratch_shapes=[dma],
+        compiler_params=pltpu.CompilerParams(vmem_limit_bytes=update_vmem),
         name="update",
     )(gradc, gradq, coef, stat, wc, wp, mc_, mp, ig)
     return (ig.reshape(block_input.shape), nwc.T, nmc.T, nwp.T, nmp.T)

time: 58.7 us -> 56.3 us (0.959)
  Pallas kernels: 57.9 us -> 55.5 us
    pallas_call x1, Pallas kernels: 3.64 us -> 1.49 us  [local(): pl.pallas_call(functools.partial(update_kernel, plan), out_shape=(sdt((nc...]
where the time goes in v3:
time: 56.3 us; the launch traced here: 56.2 us
  Pallas kernels  55.5 us (99%)
  between operations  0.67 us (1%)
    pallas_call x1, Pallas kernels, local(): pl.pallas_call(functools.partial(main_kernel, plan, names, mr, mc, gw, n)...  54 us
    pallas_call x1, Pallas kernels, local(): pl.pallas_call(functools.partial(update_kernel, plan), out_shape=(sdt((nc...  1.49 us

profile of v3, /device:TPU:0, one launch (start us, length us, event | category | flops | bytes accessed | tf_op | source)
XLA Modules:
  0.0 56.2 jit_solution(7654210021666217700)
XLA Ops:
  0.6 0.0 copy-start
  0.6 0.0 copy-start.1
  0.7 54.0 %main.1 = (bf16[512,384]{1,0:T(8,128)(2,1)S(1)}, f32[3,72,128]{2,1,0:T(8,128)S(1)}, f32[3,48,128]{2,1,0:T(8,128)S(1)}, f32[2,24,128]{2,1,0:T(8,128)S(1)}, f32[2,...) custom-call(f32[72,384]{1,0:T(8,128)} %bitcast.15, f32[24,768]{1,0:T(8,128)} %bitcast.16, ...), custom_call_target="tpu_custom_call" | custom-call | tf_op jit(solution)/shard_map/main/pallas_call | solution.py:693
  54.7 0.0 copy-done
  54.7 0.0 copy-done.1
  54.7 1.5 %update.1 = (f32[72,384]{1,0:T(8,128)}, f32[24,768]{1,0:T(8,128)}, f32[72,384]{1,0:T(8,128)}, f32[24,768]{1,0:T(8,128)}, bf16[512,384]{1,0:T(8,128)(2,1)}) custom-call(f32[3,72,128]{2,1,0:T(8,128)S(1)} %get-tuple-element.17.gradc_ref, f32[3,48,128]{2,1,0:T(8,128)S(1)} %get-tuple-element.18.gradq_ref, f32[2,24,128]{2,1,0:T(8,128)S(1)} %get-tuple-element.19.coef_ref, ...), custom_call_target="tpu_custom_call" | custom-call | tf_op jit(solution)/shard_map/update/pallas_call | solution.py:712
Async XLA Ops:
  0.6 54.1 %copy-start = (f32[384,72]{0,1:T(8,128)S(1)}, f32[384,72]{0,1:T(8,128)}, u32[]{:S(2)}) copy-start(f32[384,72]{0,1:T(8,128)} %param.12) | copy-start | bytes 331780
  0.6 54.1 %copy-start.1 = (f32[768,24]{0,1:T(8,128)S(1)}, f32[768,24]{0,1:T(8,128)}, u32[]{:S(2)}) copy-start(f32[768,24]{0,1:T(8,128)} %param.15) | copy-start | bytes 221188

commit v4 on v3

--- a/solution.py
+++ b/solution.py
@@ -329,7 +329,7 @@
                 moved = here if j == 1 else shifted(here, 1 - j, mc)
                 t.ys[pl.ds(pl.multiple_of((e + q) * mc, mc), mc), g * wide + j * gw : g * wide + (j + 1) * gw] = moved.astype(BF16)
 
-    many = next(k for k in (4, 2, 1) if mr % k == 0)
+    many = next(k for k in (8, 4, 2, 1) if mr % k == 0)
 
     def forward_all(g):
         forward(g, jnp.where(r == 1, 0, mr + 1), t.hu[...])
@@ -353,23 +353,6 @@
 
     for k in range(plan.pieces):
         spread_m(k)
-    filled, ran = [], []
-    for k in range(plan.pieces):
-        finish_m(k)
-        if k == 0:
-            continue
-        upto = k + 1 if k == plan.pieces - 1 else k
-        for q in range(k - 1, upto):
-            for side in range(2):
-                d_copy(q, side).wait()
-                unpack(plan.sets[side][q])
-                filled.append(plan.sets[side][q])
-            if sum(kind == "q" for kind, _ in filled) == plan.pieces:
-                for kind, g in filled:
-                    if kind == "c" and g not in ran:
-                        forward_all(g)
-                        ran.append(g)
-    assert len(ran) == groups
 
     part = {"c": t.pc, "q": t.pq}
     got_d = {"c": t.gdc, "q": t.gdq}
@@ -415,13 +398,14 @@
             {"batch": plan.batch(c, to, z), "rows": (r + jx) % 2},
         )
 
-    def step_m(k):
-        for side in range(2):
-            rd_copy(k, side).wait()
+    def step_m(k, side):
+        rd_copy(k, side).wait()
+        kind, g = plan.sets[side][k]
 
         def fn(rr):
             for j, jx in peers:
-                kind, g = plan.sets[(rr + jx) % 2][k]
+                if (rr + jx) % 2 != side:
+                    continue
                 first = (m + j) % nm * nz
                 two[kind][g, pl.ds(first, nz)] = (
                     part[kind][g, pl.ds(c * half + first, nz)] + got_d[kind][g, pl.ds(first, nz)]
@@ -444,8 +428,9 @@
             total = total + got_m[kind][g, i, at].astype(F32)
         return total
 
-    def step_z(k):
+    def step_z(s):
         def fn(rr):
+            k = turn[rr][s]
             for j, jx in peers:
                 rm_copy(k, j, jx, plan.sets[(rr + jx) % 2][k]).wait_send()
                 rm_copy(k, j, jx, plan.sets[rr][k]).wait_recv()
@@ -467,8 +452,9 @@
     def swap(k):
         return send(t.src2.at[k], t.other.at[k], (t.c_send, t.c_recv), k, {"batch": plan.batch(1 - c, m, z)})
 
-    def finish(k):
+    def finish(nth):
         def fn(rr):
+            k = turn[rr][nth]
             kind, g = plan.sets[rr][k]
             total = grads[kind][g]
             for j in range(1, nz):
@@ -487,7 +473,7 @@
                 t.src2[k, lead + b : lead + b + 1] = jnp.sum(off * off, axis=0, keepdims=True)
                 t.src2[k, 2 * lead + b : 2 * lead + b + 1] = jnp.sum(piece * cent, axis=0, keepdims=True)
             swap(k).start()
-            if k != order[-1]:
+            if nth < plan.pieces - 1:
                 x_copy(k, (kind, g)).start()
         by_half(r, fn)
 
@@ -535,16 +521,45 @@
             t.coef[rr, 8 + at : 8 + at + many] = gmean[0:many]
             t.coef[rr, 16 + at : 16 + at + many] = clip * coef_two
 
+    made, waiting = [], []
+
+    def drain():
+        while waiting:
+            step_m(*waiting.pop(0))
+
+    def make(k, side):
+        produce(plan.sets[side][k])
+        rd_copy(k, side).start()
+        drain()
+        waiting.append((k, side))
+        made.append((k, side))
+
+    filled = []
+    for k in range(plan.pieces):
+        finish_m(k)
+        drain()
+        if k == 0:
+            continue
+        for q in range(k - 1, k + 1 if k == plan.pieces - 1 else k):
+            for side in range(2):
+                d_copy(q, side).wait()
+                unpack(plan.sets[side][q])
+                filled.append((q, side))
+            if sum(plan.sets[side][q][0] == "q" for q, side in filled) == plan.pieces:
+                for q, side in reversed(filled):
+                    kind, g = plan.sets[side][q]
+                    if kind == "c" and (q, side) not in made:
+                        forward_all(g)
+                        make(q, side)
+    assert len(made) == groups
+    for k in reversed(range(plan.pieces)):
+        for side in range(2):
+            if plan.sets[side][k][0] == "q":
+                make(k, side)
+    drain()
+    turn = [[k for k, side in made if side == rr] for rr in range(2)]
+    assert turn[0][-1] == turn[1][-1] == 0
     order = list(reversed(range(plan.pieces)))
-    before = None
-    for k in order:
-        for side in range(2):
-            produce(plan.sets[side][k])
-            rd_copy(k, side).start()
-        if before is not None:
-            step_m(before)
-        before = k
-    step_m(before)
 
     tall = next(k for k in (2, 1) if mr % k == 0)
 
@@ -564,17 +579,15 @@
         return carry
 
     lax.fori_loop(0, mr // tall, back, 0)
-    for k in order:
-        step_z(k)
+    for s in range(plan.pieces):
+        step_z(s)
     t.src2[...] = jnp.zeros_like(t.src2)
-    ahead = []
-    for k in order:
-        finish(k)
-        if len(ahead) == 2:
-            share(ahead.pop(0))
-        ahead.append(k)
-    for k in ahead:
+    for s in range(plan.pieces - 1):
+        finish(s)
+    for k in order[:-1]:
         share(k)
+    finish(plan.pieces - 1)
+    share(order[-1])
 
     def last_x(rr):
         x_copy(order[-1], plan.sets[rr][order[-1]]).start()

time: 56.3 us -> 53.1 us (0.943)
  Pallas kernels: 55.5 us -> 52.3 us
    pallas_call x1, Pallas kernels: 54 us -> 50.8 us  [local(): pl.pallas_call(functools.partial(main_kernel, plan, names, mr, mc, gw, n)...]
where the time goes in v4:
time: 53.1 us; the launch traced here: 53 us
  Pallas kernels  52.3 us (98%)
  between operations  0.67 us (1%)
    pallas_call x1, Pallas kernels, local(): pl.pallas_call(functools.partial(main_kernel, plan, names, mr, mc, gw, n)...  50.8 us
    pallas_call x1, Pallas kernels, local(): pl.pallas_call(functools.partial(update_kernel, plan), out_shape=(sdt((nc...  1.49 us

profile of v4, /device:TPU:0, one launch (start us, length us, event | category | flops | bytes accessed | tf_op | source)
XLA Modules:
  0.0 53.0 jit_solution(5246702911320188391)
XLA Ops:
  0.6 0.0 copy-start
  0.6 0.0 copy-start.1
  0.7 50.8 %main.1 = (bf16[512,384]{1,0:T(8,128)(2,1)S(1)}, f32[3,72,128]{2,1,0:T(8,128)S(1)}, f32[3,48,128]{2,1,0:T(8,128)S(1)}, f32[2,24,128]{2,1,0:T(8,128)S(1)}, f32[2,...) custom-call(f32[72,384]{1,0:T(8,128)} %bitcast.15, f32[24,768]{1,0:T(8,128)} %bitcast.16, ...), custom_call_target="tpu_custom_call" | custom-call | tf_op jit(solution)/shard_map/main/pallas_call | solution.py:706
  51.5 0.0 copy-done
  51.5 0.0 copy-done.1
  51.5 1.5 %update.1 = (f32[72,384]{1,0:T(8,128)}, f32[24,768]{1,0:T(8,128)}, f32[72,384]{1,0:T(8,128)}, f32[24,768]{1,0:T(8,128)}, bf16[512,384]{1,0:T(8,128)(2,1)}) custom-call(f32[3,72,128]{2,1,0:T(8,128)S(1)} %get-tuple-element.17.gradc_ref, f32[3,48,128]{2,1,0:T(8,128)S(1)} %get-tuple-element.18.gradq_ref, f32[2,24,128]{2,1,0:T(8,128)S(1)} %get-tuple-element.19.coef_ref, ...), custom_call_target="tpu_custom_call" | custom-call | tf_op jit(solution)/shard_map/update/pallas_call | solution.py:725
Async XLA Ops:
  0.6 50.9 %copy-start = (f32[384,72]{0,1:T(8,128)S(1)}, f32[384,72]{0,1:T(8,128)}, u32[]{:S(2)}) copy-start(f32[384,72]{0,1:T(8,128)} %param.12) | copy-start | bytes 331780
  0.6 50.9 %copy-start.1 = (f32[768,24]{0,1:T(8,128)S(1)}, f32[768,24]{0,1:T(8,128)}, u32[]{:S(2)}) copy-start(f32[768,24]{0,1:T(8,128)} %param.15) | copy-start | bytes 221188
